TPU v7x, 32 devices: a whole 2x2x4 slice. The times are simulated.
32 devices in a mesh: gx: 4 (over z), gy: 2 (over x), gz: 4 (over y, core).
Axes of the slice: x: 2, y: 2, z: 4, core: 2. Of those that a mesh axis runs over, the one named last changes fastest.
Arguments:
- block_x: float32 [16, 24, 12, 512], P(None, 'gz', 'gy', 'gx')
- block_hx: float32 [16, 24, 12, 512], P(None, 'gz', 'gy', 'gx')
- block_p: float32 [16, 24, 12, 512], P(None, 'gz', 'gy', 'gx')
- block_hp: float32 [16, 24, 12, 512], P(None, 'gz', 'gy', 'gx')
- potential: float32 [24, 12, 512], P('gz', 'gy', 'gx'), may hold values from -2 to 2
- projectors: float32 [4, 2, 4, 8, 4, 256], P('gz', 'gy', 'gx'), may hold values from -0.75 to 0.75
- coupling: float32 [4, 2, 4, 8, 4, 4], P('gz', 'gy', 'gx'), may hold values from 0.25 to 1.25
- atom_count: int32 [4, 2, 4], P('gz', 'gy', 'gx'), may hold values from 0 to 8, as said below
- proj_count: int32 [4, 2, 4, 8], P('gz', 'gy', 'gx'), may hold values from 1 to 4
- offsets: int32 [3, 4, 2, 4, 8], P(None, 'gz', 'gy', 'gx'), may hold values from 0 to 127, as said below
- extents: int32 [3, 4, 2, 4, 8], P(None, 'gz', 'gy', 'gx'), may hold values from 2 to 16, as said below
Outputs:
- w_block: float32 [16, 24, 12, 512], P(None, 'gz', 'gy', 'gx')
- hw_block: float32 [16, 24, 12, 512], P(None, 'gz', 'gy', 'gx')
- gram: float32 [48, 48], replicated
- rayleigh: float32 [48, 48], replicated
Inputs may be any that keep to these rules, and one draw needn't show every extreme that they name: `atom_count`: slots at and above a domain's count are empty; some domain is full in every draw. The first proj_count projectors of a slot are used. `offsets`: components z, y, x are below 6, 6, 128. `extents`: components z, y, x are at most 4, 4, 16; some slot has the full box in every draw.
All inputs are finite; a program needn't handle non-finite values.
Results may differ from a plain program's by a relative error of at most 0.0003.
Values sent between devices are 32-bit elements; how exact they have to be, the bound alone decides.
A program may use at most 64 MiB of HBM per device.

v0:
```python
import jax
import jax.numpy as jnp
from jax import lax
from jax.sharding import PartitionSpec as P

BZ = 4
BY = 4
BX = 16


LAP_CENTER = -5369.0 / 1800.0
LAP_COEFFS = (12.0 / 7.0, -15.0 / 56.0, 10.0 / 189.0, -1.0 / 112.0, 2.0 / 1925.0, -1.0 / 16632.0)
HIGHEST = lax.Precision.HIGHEST


def shifted(value, axis, steps):
    count = lax.axis_size(axis)
    pairs = [(source, (source + steps) % count) for source in range(count)]
    return lax.ppermute(value, axis, pairs)


def with_halo(x, sides, width):
    for axis, dim in sides:
        peers, length = (lax.axis_size(axis), x.shape[dim])
        up = [(i, (i + 1) % peers) for i in range(peers)]
        down = [(j, i) for i, j in up]
        last = lax.slice_in_dim(x, length - width, length, axis=dim)
        first = lax.slice_in_dim(x, 0, width, axis=dim)
        before = lax.ppermute(last, axis, up)
        after = lax.ppermute(first, axis, down)
        x = jnp.concatenate([before, x, after], axis=dim)
    return x


def masked_projectors(projectors, atom_count, proj_count, extents):
    slot_index = jnp.arange(projectors.shape[-3], dtype=jnp.int32)
    live_slot = slot_index < atom_count[..., None]
    proj_index = jnp.arange(projectors.shape[-2], dtype=jnp.int32)
    live_proj = proj_index < proj_count[..., None]
    cell_index = jnp.arange(projectors.shape[-1], dtype=jnp.int32)
    along_z = cell_index // (BY * BX)
    along_y = cell_index // BX % BY
    along_x = cell_index % BX
    inside = (
        (along_z < extents[0][..., None])
        & (along_y < extents[1][..., None])
        & (along_x < extents[2][..., None])
    )
    keeper = live_slot[..., None, None] & live_proj[..., None] & inside[..., None, :]
    return jnp.where(keeper, projectors, jnp.zeros_like(projectors))


def kinetic_from(padded, column_block, depth):
    size_z, size_y, size_x = (column_block.shape[1], column_block.shape[2], column_block.shape[3])
    summed = 3.0 * LAP_CENTER * column_block
    for distance, weight in enumerate(LAP_COEFFS, start=1):
        beside_all = padded[
            :,
            depth + distance : depth + distance + size_z,
            depth : depth + size_y,
            depth : depth + size_x,
        ]
        beside_all = (
            beside_all
            + padded[
                :,
                depth - distance : depth - distance + size_z,
                depth : depth + size_y,
                depth : depth + size_x,
            ]
        )
        beside_all = (
            beside_all
            + padded[
                :,
                depth : depth + size_z,
                depth + distance : depth + distance + size_y,
                depth : depth + size_x,
            ]
        )
        beside_all = (
            beside_all
            + padded[
                :,
                depth : depth + size_z,
                depth - distance : depth - distance + size_y,
                depth : depth + size_x,
            ]
        )
        beside_all = (
            beside_all
            + padded[
                :,
                depth : depth + size_z,
                depth : depth + size_y,
                depth + distance : depth + distance + size_x,
            ]
        )
        beside_all = (
            beside_all
            + padded[
                :,
                depth : depth + size_z,
                depth : depth + size_y,
                depth - distance : depth - distance + size_x,
            ]
        )
        summed = summed + weight * beside_all
    return -0.5 * summed


def cut_boxes(frame_block, corners):
    columns = frame_block.shape[0]

    def cut_single(corner_cell):
        window = lax.dynamic_slice(
            frame_block,
            (jnp.int32(0), corner_cell[0], corner_cell[1], corner_cell[2]),
            (columns, BZ, BY, BX),
        )
        return window.reshape(columns, BZ * BY * BX)

    return jax.vmap(cut_single)(corners)


def deposit_boxes(frame_block, corners, pieces):
    columns = frame_block.shape[0]

    def add_single(slot_number, current):
        corner_cell = corners[slot_number]
        position = (jnp.int32(0), corner_cell[0], corner_cell[1], corner_cell[2])
        previous = lax.dynamic_slice(current, position, (columns, BZ, BY, BX))
        updated = previous + pieces[slot_number].reshape(columns, BZ, BY, BX)
        return lax.dynamic_update_slice(current, updated, position)

    return lax.fori_loop(0, corners.shape[0], add_single, frame_block)


def boxes_and_fold(frame_block, beta_masked, sym_coupling, starts, size_z, size_y, size_x):
    box_values = cut_boxes(frame_block, starts)
    correlations = jnp.einsum("spk,snk->spn", beta_masked, box_values, precision=HIGHEST)
    weights_out = jnp.einsum("spq,sqn->spn", sym_coupling, correlations, precision=HIGHEST)
    pieces = jnp.einsum("spk,spn->snk", beta_masked, weights_out, precision=HIGHEST)
    spread = deposit_boxes(jnp.zeros_like(frame_block), starts, pieces)
    spill_over = shifted(spread[:, :, :, size_x:], "gx", 1)
    spread = spread[:, :, :, :size_x]
    spread = jnp.concatenate([spread[:, :, :, :BX] + spill_over, spread[:, :, :, BX:]], axis=3)
    spill_over = shifted(spread[:, :, size_y:], "gy", 1)
    spread = spread[:, :, :size_y]
    spread = jnp.concatenate([spread[:, :, :BY] + spill_over, spread[:, :, BY:]], axis=2)
    spill_over = shifted(spread[:, size_z:], "gz", 1)
    spread = spread[:, :size_z]
    return jnp.concatenate([spread[:, :BZ] + spill_over, spread[:, BZ:]], axis=1)


def frame_by_fields(column_block):
    frame_block = column_block
    upper_slab = shifted(frame_block[:, :BZ], "gz", -1)
    frame_block = jnp.concatenate([frame_block, upper_slab], axis=1)
    upper_slab = shifted(frame_block[:, :, :BY], "gy", -1)
    frame_block = jnp.concatenate([frame_block, upper_slab], axis=2)
    upper_slab = shifted(frame_block[:, :, :, :BX], "gx", -1)
    return jnp.concatenate([frame_block, upper_slab], axis=3)


def inner_product(left_block, right_block):
    left_flat = left_block.reshape(left_block.shape[0], -1)
    right_flat = right_block.reshape(right_block.shape[0], -1)
    return jnp.einsum("ic,jc->ij", left_flat, right_flat, precision=HIGHEST)


def per_device(
    block_x,
    block_hx,
    block_p,
    block_hp,
    potential,
    projectors,
    coupling,
    atom_count,
    proj_count,
    offsets,
    extents,
):
    columns = block_x.shape[0]
    size_z, size_y, size_x = (block_x.shape[1], block_x.shape[2], block_x.shape[3])
    cell_weight = 1.0 / (
        size_z * size_y * size_x * lax.axis_size("gx") * lax.axis_size("gy") * lax.axis_size("gz")
    )
    beta_masked = masked_projectors(projectors, atom_count, proj_count, extents)[0, 0, 0]
    sym_coupling = (0.5 * (coupling + jnp.swapaxes(coupling, -1, -2)))[0, 0, 0]
    starts = jnp.transpose(offsets[:, 0, 0, 0, :])
    correlation, projected = lax.psum(
        (inner_product(block_x, block_x), inner_product(block_x, block_hx)), ("gx", "gy", "gz")
    )
    correlation = correlation * cell_weight
    projected = projected * cell_weight
    factor = jnp.linalg.cholesky(correlation)
    ritz_theta = jax.scipy.linalg.cho_solve((factor, True), projected)
    residual = block_hx - jnp.einsum("kzyx,kj->jzyx", block_x, ritz_theta, precision=HIGHEST)
    w_block = residual / (1.0 + potential * potential)
    stencil_reach = len(LAP_COEFFS)
    padded = with_halo(w_block, (("gx", 3), ("gy", 2), ("gz", 1)), stencil_reach)
    kinetic_part = kinetic_from(padded, w_block, stencil_reach)
    frame_block = frame_by_fields(w_block)
    nonlocal_part = boxes_and_fold(
        frame_block, beta_masked, sym_coupling, starts, size_z, size_y, size_x
    )
    hw_block = kinetic_part + potential * w_block + nonlocal_part
    search_space = jnp.concatenate([block_x, w_block, block_p], axis=0)
    pair_wp = jnp.concatenate([w_block, block_p], axis=0)
    gram_w, gram_p, ray_w, ray_p, ray_x = lax.psum(
        (
            inner_product(search_space, w_block),
            inner_product(search_space, block_p),
            inner_product(search_space, hw_block),
            inner_product(search_space, block_hp),
            inner_product(pair_wp, block_hx),
        ),
        ("gx", "gy", "gz"),
    )
    gram_w = gram_w * cell_weight
    gram_p = gram_p * cell_weight
    ray_w = ray_w * cell_weight
    ray_p = ray_p * cell_weight
    ray_x = ray_x * cell_weight
    gram = jnp.block(
        [
            [correlation, gram_w[:columns], gram_p[:columns]],
            [gram_w[:columns].T, gram_w[columns : 2 * columns], gram_p[columns : 2 * columns]],
            [gram_p[:columns].T, gram_w[2 * columns :], gram_p[2 * columns :]],
        ]
    )
    rayleigh = jnp.block(
        [
            [projected, ray_w[:columns], ray_p[:columns]],
            [ray_x[:columns], ray_w[columns : 2 * columns], ray_p[columns : 2 * columns]],
            [ray_x[columns:], ray_w[2 * columns :], ray_p[2 * columns :]],
        ]
    )
    return (w_block, hw_block, gram, rayleigh)


def solution(mesh):
    in_specs = (
        P(None, "gz", "gy", "gx"),
        P(None, "gz", "gy", "gx"),
        P(None, "gz", "gy", "gx"),
        P(None, "gz", "gy", "gx"),
        P("gz", "gy", "gx"),
        P("gz", "gy", "gx", None, None, None),
        P("gz", "gy", "gx", None, None, None),
        P("gz", "gy", "gx"),
        P("gz", "gy", "gx", None),
        P(None, "gz", "gy", "gx", None),
        P(None, "gz", "gy", "gx", None),
    )
    out_specs = (P(None, "gz", "gy", "gx"), P(None, "gz", "gy", "gx"), P(), P())
    return jax.shard_map(
        per_device, mesh=mesh, in_specs=in_specs, out_specs=out_specs, check_vma=False
    )
```

profile of v0, /device:TPU:0, one launch (start us, length us, event | category | flops | bytes accessed | tf_op | source)
XLA Modules:
  0.0 322.8 jit_solution(12400363442341101703)
XLA Ops:
  3.9 42.1 %all-reduce.1 = (f32[16,16]{0,1:T(8,128)S(1)}, f32[16,16]{0,1:T(8,128)S(1)}) all-reduce(f32[16,16]{0,1:T(8,128)S(1)} %convolution_bitcast_fusion.7, f32[16,16]{0,1:T(8,128)S(1)} %convolution_bitcast_fusion.6), channel_id=1, replica_groups=mesh['gx'=4,'gy'=2,'gz'=4] {'gx','gy','gz'}, use_global_device_ids=true, to_apply=%region_0.1 | all-reduce | flops 512 | bytes 4096 | tf_op jit(solution)/shard_map/psum | solution.py:193
  53.8 2.2 collective-permute-start.1
  57.7 2.3 collective-permute-start.7
  60.2 8.4 %collective-permute-done.7 = f32[16,10,4,128]{3,0,2,1:T(8,128)S(1)} collective-permute-done((f32[16,10,4,128]{3,0,2,1:T(8,128)S(1)}, f32[16,10,4,128]{3,0,2,1:T(8,128)S(1)}, u32[]{:S(2)}, u32[]{:S(2)}) %collective-permute-start.7) | collective-permute-done | bytes 327712 | tf_op jit(solution)/shard_map/ppermute | solution.py:19
  68.7 3.1 collective-permute-start.8
  71.8 17.2 %collective-permute-done.8 = f32[16,10,10,16]{3,0,2,1:T(8,128)S(1)} collective-permute-done((f32[16,10,10,16]{3,0,2,1:T(8,128)S(1)}, f32[16,10,10,16]{3,0,2,1:T(8,128)S(1)}, u32[]{:S(2)}, u32[]{:S(2)}) %collective-permute-start.8) | collective-permute-done | bytes 102432 | tf_op jit(solution)/shard_map/ppermute | solution.py:19
  89.1 26.8 %while.15 = (s32[]{:T(128)}, f32[16,10,10,144]{3,0,2,1:T(8,128)S(1)}, s32[8,4]{0,1:T(4,128)S(1)}, f32[8,16,4,4,16]{4,3,2,1,0:T(4,128)}, s32[]{:T(128)}) while((s32[]{:T(128)}, f32[16,10,10,144]{3,0,2,1:T(8,128)S(1)}, s32[8,4]{0,1:T(4,128)S(1)}, f32[8,16,4,4,16]{4,3,2,1,0:T(4,128)}, s32[]{:T(128)}) %tuple.73), condition=%wide.while_cond, body=%wide.while_body.sunk | while | flops 2 | bytes 180369 | solution.py:116
  89.8 2.0 constant_dynamic-slice_fusion.14
  93.2 2.0 constant_dynamic-slice_fusion.14
  96.5 2.0 constant_dynamic-slice_fusion.14
  99.9 2.0 constant_dynamic-slice_fusion.14
  103.2 2.0 constant_dynamic-slice_fusion.14
  106.6 2.0 constant_dynamic-slice_fusion.14
  109.9 2.0 constant_dynamic-slice_fusion.14
  113.3 2.0 constant_dynamic-slice_fusion.14
  116.0 2.1 reshape.274
  119.1 74.6 %while.14 = (s32[]{:T(128)}, f32[16,10,10,144]{3,0,2,1:T(8,128)S(1)}, s32[8,3]{0,1:T(4,128)S(1)}, f32[8,16,256]{2,1,0:T(8,128)S(1)}, s32[]{:T(128)}, /*index=5*/s32[]{:T(128)}, s32[]{:T(128)}, s32[]{:T(128)}) while((s32[]{:T(128)}, f32[16,10,10,144]{3,0,2,1:T(8,128)S(1)}, s32[8,3]{0,1:T(4,128)S(1)}, f32[8,16,256]{2,1,0:T(8,128)S(1)}, ...), condition=%wide.region_5.6_spmd, body=%wide.region_4.5_spmd.sunk | while | flops 4107 | bytes 213259 | solution.py:136
  125.9 2.6 dynamic_update_slice.8
  135.2 2.6 dynamic_update_slice.8
  144.5 2.6 dynamic_update_slice.8
  153.8 2.6 dynamic_update_slice.8
  163.2 2.6 dynamic_update_slice.8
  172.5 2.6 dynamic_update_slice.8
  181.8 2.6 dynamic_update_slice.8
  191.2 2.6 dynamic_update_slice.8
  198.7 16.4 %collective-permute-done.9 = f32[16,10,10,16]{3,0,2,1:T(8,128)S(1)} collective-permute-done((f32[16,10,10,16]{3,0,2,1:T(8,128)S(1)}, f32[16,10,10,16]{3,0,2,1:T(8,128)S(1)}, u32[]{:S(2)}, u32[]{:S(2)}) %collective-permute-start.9) | collective-permute-done | bytes 102432 | tf_op jit(solution)/shard_map/ppermute | solution.py:19
  215.4 3.1 collective-permute-start.10
  219.3 5.9 %collective-permute-done.2 = f32[16,6,6,140]{3,0,2,1:T(8,128)S(1)} collective-permute-done((f32[16,6,6,140]{3,0,2,1:T(8,128)S(1)}, f32[16,6,6,140]{3,0,2,1:T(8,128)S(1)}, u32[]{:S(2)}, u32[]{:S(2)}) %collective-permute-start.2) | collective-permute-done | bytes 322592 | tf_op jit(solution)/shard_map/ppermute | solution.py:29
  226.8 1.7 collective-permute-start.4
  232.9 37.3 %collective-permute-done.11 = f32[16,4,6,128]{3,0,2,1:T(8,128)} collective-permute-done((f32[16,4,6,128]{3,0,2,1:T(8,128)}, f32[16,4,6,128]{3,0,2,1:T(8,128)}, u32[]{:S(2)}, u32[]{:S(2)}) %collective-permute-start.11) | collective-permute-done | bytes 196640 | tf_op jit(solution)/shard_map/ppermute | solution.py:19
  271.2 7.2 %fusion.16 = f32[16,6,6,128]{3,0,2,1:T(8,128)S(1)} fusion(f32[16,6,6,6]{3,0,2,1:T(8,128)S(1)} %copy-done.6, f32[16,6,6,128]{3,0,2,1:T(8,128)S(1)} %fusion.1, f32[16,6,6,6]{3,0,2,1:T(8,128)S(1)} %collective-permute-done.1, f32[16,6,6,140]{3,0,2,1:T(8,128)S(1)} %copy-done.4, f32[16,6,6,140]{3,0,2,1:T(8,128)S(1)} %collective-permute-done.3, ...), kind=kLoop, calls=%fused_computation.68 | loop fusion | flops 8110080 | bytes 10346496 | tf_op jit(solution)/shard_map/add | solution.py:209
  279.2 40.8 %all-reduce = (f32[48,16]{0,1:T(8,128)S(1)}, f32[48,16]{0,1:T(8,128)S(1)}, f32[48,16]{0,1:T(8,128)S(1)}, f32[48,16]{0,1:T(8,128)S(1)}, f32[32,16]{0,1:T(8,128)S(1)}) all-reduce(f32[48,16]{0,1:T(8,128)S(1)} %convolution_bitcast_fusion.3, ...), channel_id=1, replica_groups=mesh['gx'=4,'gy'=2,'gz'=4] {'gx','gy','gz'}, use_global_device_ids=true, to_apply=%region_7.8 | all-reduce | flops 3584 | bytes 28672 | tf_op jit(solution)/shard_map/psum | solution.py:212
  (210 shorter events, 48.8 us)
Async XLA Ops:
  0.6 227.9 %copy-start = (f32[16,6,6,128]{3,0,2,1:T(8,128)S(1)}, f32[16,6,6,128]{3,0,2,1:T(8,128)}, u32[]{:S(2)}) copy-start(f32[16,6,6,128]{3,0,2,1:T(8,128)} %param.16) | copy-start | bytes 884740
  2.2 54.4 %copy-start.16 = (s32[3,1,1,1,8]{4,3,2,1,0:T(1,128)S(1)}, s32[3,1,1,1,8]{4,3,2,1,0:T(1,128)}, u32[]{:S(2)}) copy-start(s32[3,1,1,1,8]{4,3,2,1,0:T(1,128)} %param.23) | copy-start | bytes 292
  2.2 54.4 %copy-start.15 = (s32[3,1,1,1,8]{4,3,2,1,0:T(1,128)S(1)}, s32[3,1,1,1,8]{4,3,2,1,0:T(1,128)}, u32[]{:S(2)}) copy-start(s32[3,1,1,1,8]{4,3,2,1,0:T(1,128)} %param.22) | copy-start | bytes 292
  2.2 54.5 %copy-start.14 = (f32[1,1,1,8,4,4]{3,5,4,2,1,0:T(4,128)S(1)}, f32[1,1,1,8,4,4]{3,5,4,2,1,0:T(4,128)}, u32[]{:S(2)}) copy-start(f32[1,1,1,8,4,4]{3,5,4,2,1,0:T(4,128)} %param.19) | copy-start | bytes 1540
  2.3 54.6 %copy-start.2 = (f32[16,6,6,128]{3,0,2,1:T(8,128)S(1)}, f32[16,6,6,128]{3,0,2,1:T(8,128)}, u32[]{:S(2)}) copy-start(f32[16,6,6,128]{3,0,2,1:T(8,128)} %param.13) | copy-start | bytes 884740
  2.3 54.6 %copy-start.7 = (f32[16,6,6,128]{3,0,2,1:T(8,128)S(1)}, f32[16,6,6,128]{3,0,2,1:T(8,128)}, u32[]{:S(2)}) copy-start(f32[16,6,6,128]{3,0,2,1:T(8,128)} %param.15) | copy-start | bytes 884740
  52.7 225.6 %copy-start.1 = (f32[16,6,6,128]{3,0,2,1:T(8,128)}, f32[16,6,6,128]{3,0,2,1:T(8,128)S(1)}, u32[]{:S(2)}) copy-start(f32[16,6,6,128]{3,0,2,1:T(8,128)S(1)} %fusion.1) | copy-start | bytes 884740
  52.7 4.9 %copy-start.17 = (s32[1,1,1,8]{3,2,1,0:T(1,128)S(1)}, s32[1,1,1,8]{3,2,1,0:T(1,128)}, u32[]{:S(2)}) copy-start(s32[1,1,1,8]{3,2,1,0:T(1,128)} %param.21) | copy-start | bytes 100
  52.8 4.9 %collective-permute-start.6 = (f32[16,4,6,128]{3,0,2,1:T(8,128)S(1)}, f32[16,4,6,128]{3,0,2,1:T(8,128)S(1)}, u32[]{:S(2)}, u32[]{:S(2)}) collective-permute-start(f32[16,4,6,128]{3,0,2,1:T(8,128)S(1)} %slice.420), channel_id=1, source_target_pairs={{0,3},{1,0},{2,1},{3,2},{4,7},{5,4},{6,5},{7,6},{8,11},{9,8},{10,9... | collective-permute-start | bytes 589832 | tf_op jit(solution)/shard_map/ppermute | solution.py:19
  53.8 141.5 %collective-permute-start.1 = (f32[16,6,6,6]{3,0,2,1:T(8,128)}, f32[16,6,6,6]{3,0,2,1:T(8,128)S(1)}, u32[]{:S(2)}, u32[]{:S(2)}) collective-permute-start(f32[16,6,6,6]{3,0,2,1:T(8,128)} %get-tuple-element.135), channel_id=1, source_target_pairs={{8,0},{16,8},{24,16},{0,24},{9,1},{17,9},{25,17},{1,25},{10,2},{18... | collective-permute-start | bytes 41480 | tf_op jit(solution)/shard_map/ppermute | solution.py:30
  56.0 139.3 %collective-permute-start = (f32[16,6,6,6]{3,0,2,1:T(8,128)}, f32[16,6,6,6]{3,0,2,1:T(8,128)S(1)}, u32[]{:S(2)}, u32[]{:S(2)}) collective-permute-start(f32[16,6,6,6]{3,0,2,1:T(8,128)} %get-tuple-element.136), channel_id=1, source_target_pairs={{0,8},{8,16},{16,24},{24,0},{1,9},{9,17},{17,25},{25,1},{2,10},{10... | collective-permute-start | bytes 41480 | tf_op jit(solution)/shard_map/ppermute | solution.py:29
  57.7 10.9 %collective-permute-start.7 = (f32[16,10,4,128]{3,0,2,1:T(8,128)S(1)}, f32[16,10,4,128]{3,0,2,1:T(8,128)S(1)}, u32[]{:S(2)}, u32[]{:S(2)}) collective-permute-start(f32[16,10,4,128]{3,0,2,1:T(8,128)S(1)} %pad_maximum_fusion.11), channel_id=1, source_target_pairs={{0,4},{4,0},{1,5},{5,1},{2,6},{6,2},{3,7},{7,3},{8,12},{12,8},{9,1... | collective-permute-start | bytes 983048 | tf_op jit(solution)/shard_map/ppermute | solution.py:19
  68.7 20.3 %collective-permute-start.8 = (f32[16,10,10,16]{3,0,2,1:T(8,128)S(1)}, f32[16,10,10,16]{3,0,2,1:T(8,128)S(1)}, u32[]{:S(2)}, u32[]{:S(2)}) collective-permute-start(f32[16,10,10,16]{3,0,2,1:T(8,128)S(1)} %pad_maximum_fusion.4), channel_id=1, source_target_pairs={{0,24},{8,0},{16,8},{24,16},{1,25},{9,1},{17,9},{25,17},{2,26},{10... | collective-permute-start | bytes 307208 | tf_op jit(solution)/shard_map/ppermute | solution.py:19
  89.1 28.9 %copy-start.12 = (f32[1,1,1,8,4,256]{5,4,3,2,1,0:T(4,128)S(1)}, f32[1,1,1,8,4,256]{5,4,3,2,1,0:T(4,128)}, u32[]{:S(2)}) copy-start(f32[1,1,1,8,4,256]{5,4,3,2,1,0:T(4,128)} %param.18) | copy-start | bytes 98308
  193.9 21.3 %collective-permute-start.9 = (f32[16,10,10,16]{3,0,2,1:T(8,128)S(1)}, f32[16,10,10,16]{3,0,2,1:T(8,128)S(1)}, u32[]{:S(2)}, u32[]{:S(2)}) collective-permute-start(f32[16,10,10,16]{3,0,2,1:T(8,128)S(1)} %slice.343), channel_id=1, source_target_pairs={{0,8},{8,16},{16,24},{24,0},{1,9},{9,17},{17,25},{25,1},{2,10},{10... | collective-permute-start | bytes 307208 | tf_op jit(solution)/shard_map/ppermute | solution.py:19
  195.3 0.7 copy-start.5
  196.3 23.0 %collective-permute-start.3 = (f32[16,6,6,140]{3,0,2,1:T(8,128)S(1)}, f32[16,6,6,140]{3,0,2,1:T(8,128)S(1)}, u32[]{:S(2)}, u32[]{:S(2)}) collective-permute-start(f32[16,6,6,140]{3,0,2,1:T(8,128)S(1)} %pad_maximum_fusion.6), channel_id=1, source_target_pairs={{4,0},{0,4},{5,1},{1,5},{6,2},{2,6},{7,3},{3,7},{12,8},{8,12},{13,... | collective-permute-start | bytes 967688 | tf_op jit(solution)/shard_map/ppermute | solution.py:30
  197.8 27.4 %collective-permute-start.2 = (f32[16,6,6,140]{3,0,2,1:T(8,128)S(1)}, f32[16,6,6,140]{3,0,2,1:T(8,128)S(1)}, u32[]{:S(2)}, u32[]{:S(2)}) collective-permute-start(f32[16,6,6,140]{3,0,2,1:T(8,128)S(1)} %pad_maximum_fusion.6), channel_id=1, source_target_pairs={{0,4},{4,0},{1,5},{5,1},{2,6},{6,2},{3,7},{7,3},{8,12},{12,8},{9,1... | collective-permute-start | bytes 967688 | tf_op jit(solution)/shard_map/ppermute | solution.py:29
  198.7 19.8 %copy-start.8 = (f32[16,6,6,128]{3,0,2,1:T(8,128)S(1)}, f32[16,6,6,128]{3,0,2,1:T(8,128)}, u32[]{:S(2)}) copy-start(f32[16,6,6,128]{3,0,2,1:T(8,128)} %param.15) | copy-start | bytes 884740
  215.3 10.0 %copy-start.6 = (f32[16,6,6,6]{3,0,2,1:T(8,128)S(1)}, f32[16,6,6,6]{3,0,2,1:T(8,128)}, u32[]{:S(2)}) copy-start(f32[16,6,6,6]{3,0,2,1:T(8,128)} %copy-done.5) | copy-start | bytes 41476
  215.4 15.1 %collective-permute-start.10 = (f32[16,10,4,128]{3,0,2,1:T(8,128)S(1)}, f32[16,10,4,128]{3,0,2,1:T(8,128)S(1)}, u32[]{:S(2)}, u32[]{:S(2)}) collective-permute-start(f32[16,10,4,128]{3,0,2,1:T(8,128)S(1)} %fusion.6), channel_id=1, source_target_pairs={{0,4},{4,0},{1,5},{5,1},{2,6},{6,2},{3,7},{7,3},{8,12},{12,8},{9,1... | collective-permute-start | bytes 983048 | tf_op jit(solution)/shard_map/ppermute | solution.py:19
  225.2 1.6 copy-start.3
  226.8 44.3 %collective-permute-start.5 = (f32[16,6,18,140]{3,0,2,1:T(8,128)}, f32[16,6,18,140]{3,0,2,1:T(8,128)}, u32[]{:S(2)}, u32[]{:S(2)}) collective-permute-start(f32[16,6,18,140]{3,0,2,1:T(8,128)} %pad_maximum_fusion), channel_id=1, source_target_pairs={{0,1},{1,2},{2,3},{3,0},{4,5},{5,6},{6,7},{7,4},{8,9},{9,10},{10,1... | collective-permute-start | bytes 2903048 | tf_op jit(solution)/shard_map/ppermute | solution.py:29
  226.8 44.3 %collective-permute-start.4 = (f32[16,6,18,140]{3,0,2,1:T(8,128)}, f32[16,6,18,140]{3,0,2,1:T(8,128)}, u32[]{:S(2)}, u32[]{:S(2)}) collective-permute-start(f32[16,6,18,140]{3,0,2,1:T(8,128)} %pad_maximum_fusion), channel_id=1, source_target_pairs={{1,0},{2,1},{3,2},{0,3},{5,4},{6,5},{7,6},{4,7},{9,8},{10,9},{11,1... | collective-permute-start | bytes 2903048 | tf_op jit(solution)/shard_map/ppermute | solution.py:30
  230.7 1.0 copy-start.11
  230.7 1.6 copy-start.4
  231.5 38.7 %collective-permute-start.11 = (f32[16,4,6,128]{3,0,2,1:T(8,128)}, f32[16,4,6,128]{3,0,2,1:T(8,128)}, u32[]{:S(2)}, u32[]{:S(2)}) collective-permute-start(f32[16,4,6,128]{3,0,2,1:T(8,128)} %slice.426), channel_id=1, source_target_pairs={{0,1},{1,2},{2,3},{3,0},{4,5},{5,6},{6,7},{7,4},{8,9},{9,10},{10,1... | collective-permute-start | bytes 589832 | tf_op jit(solution)/shard_map/ppermute | solution.py:19
  232.3 38.9 %copy-start.13 = (f32[6,6,128]{2,1,0:T(8,128)S(1)}, f32[6,6,128]{2,1,0:T(8,128)}, u32[]{:S(2)}) copy-start(f32[6,6,128]{2,1,0:T(8,128)} %param.17) | copy-start | bytes 55300
  271.1 7.2 %copy-start.9 = (f32[16,6,6,128]{3,0,2,1:T(8,128)S(1)}, f32[16,6,6,128]{3,0,2,1:T(8,128)}, u32[]{:S(2)}) copy-start(f32[16,6,6,128]{3,0,2,1:T(8,128)} %param.15) | copy-start | bytes 884740
  278.4 44.4 %copy-start.10 = (f32[16,6,6,128]{3,0,2,1:T(8,128)}, f32[16,6,6,128]{3,0,2,1:T(8,128)S(1)}, u32[]{:S(2)}) copy-start(f32[16,6,6,128]{3,0,2,1:T(8,128)S(1)} %fusion.16) | copy-start | bytes 884740
where the time goes:
time: 324 us; the launch traced here: 323 us
  waiting for transfers between devices  86.4 us (27%)
  blocking collectives  82.9 us (26%)
  local copies, waits for them, and re-layouts  62 us (19%)
  loops' own time  45.6 us (14%)
  other arithmetic  18.4 us (6%)
  starting transfers between devices  16.1 us (5%)
  matrix products  9.65 us (3%)
    ppermute x6, waiting for transfers between devices, shifted(): return lax.ppermute(value, axis, pairs)  80.5 us
    another operation x1, loops' own time, deposit_boxes(): return lax.fori_loop(0, corners.shape[0], add_single, frame_block)  45.5 us
    psum x1, blocking collectives, per_device(): lax.psum((inner_product(block_x, block_x), inner_product(block_x, block_h...  42.1 us
    psum x1, blocking collectives, per_device(): lax.psum((inner_product(search_space, w_block), inner_product(search_spac...  40.8 us
    gather x32, local copies, waits for them, and re-layouts  26.7 us
    dynamic_update_slice x16, local copies, waits for them, and re-layouts, add_single(): return lax.dynamic_update_slice(current, updated, position)  21.2 us
    ppermute x6, starting transfers between devices, shifted(): return lax.ppermute(value, axis, pairs)  10 us
    add x1, other arithmetic, per_device(): hw_block = kinetic_part + potential * w_block + nonlocal_part  7.21 us
  transfers between devices with their start and end apart: 12, of which 6 were waited for; matrix products, arithmetic and copies ran while one was open for 21% of the time, Pallas kernels for 0%

commit v1 on v0

v1 whole, which is shorter than its diff:
```python
import functools

import jax
import jax.numpy as jnp
from jax import lax
from jax.experimental import pallas as pl
from jax.experimental.pallas import tpu as pltpu
from jax.sharding import PartitionSpec as P

BZ, BY, BX = 4, 4, 16
LAP_CENTER = -5369.0 / 1800.0
LAP_COEFFS = (12.0 / 7.0, -15.0 / 56.0, 10.0 / 189.0, -1.0 / 112.0, 2.0 / 1925.0, -1.0 / 16632.0)
MESH = pl.DeviceIdType.MESH
AXES = ("gz", "gy", "gx")
F32 = jnp.float32
BF16 = jnp.bfloat16
HX, HP, XX, PP, WW, HW = range(6)


def masked_projectors(projectors, atom_count, proj_count, extents):
    slot_index = jnp.arange(projectors.shape[-3], dtype=jnp.int32)
    live_slot = slot_index < atom_count[..., None]
    proj_index = jnp.arange(projectors.shape[-2], dtype=jnp.int32)
    live_proj = proj_index < proj_count[..., None]
    cell_index = jnp.arange(projectors.shape[-1], dtype=jnp.int32)
    along_z = cell_index // (BY * BX)
    along_y = cell_index // BX % BY
    along_x = cell_index % BX
    inside = (
        (along_z < extents[0][..., None])
        & (along_y < extents[1][..., None])
        & (along_x < extents[2][..., None])
    )
    keeper = live_slot[..., None, None] & live_proj[..., None] & inside[..., None, :]
    return jnp.where(keeper, projectors, jnp.zeros_like(projectors))


def tiles_of(count):
    return -(-count // 8)


def kernel(
    sizes, groups, dims,
    off_ref, d_ref, x_ref, hx_ref, p_ref, hp_ref, v_ref, beta_ref,
    w_ref, hw_ref, red1_ref, red2_ref,
    stack, zext, ybuf, zybuf, plow, phigh, xr, xl, frame, frame_x, halo_x,
    blo, bhi, pieces, nf, nh, spack, rz, ry, rzy, rx, wout,
    *rest,
):
    cz, cy, cx, slots, nproj, cols = dims
    nz, ny, nx = sizes
    n_red = len(groups)
    bufs = (rest[:n_red], rest[n_red : 2 * n_red])
    rest = rest[2 * n_red :]
    red_send, red_recv, halo_send, halo_recv, spill_send, spill_recv = rest
    zi, yi, xi = (lax.axis_index(a) for a in AXES)
    size_of = dict(zip(AXES, sizes))
    here = dict(zip(AXES, (zi, yi, xi)))
    fz, fy = cz + BZ - 1, cy + BY - 1
    own = cz * cy
    lane = lax.broadcasted_iota(jnp.int32, (cols, 128), 1)

    def neighbour(dz, dy, dx):
        step = dict(zip(AXES, (dz, dy, dx)))
        return {a: lax.rem(here[a] + step[a] + size_of[a], size_of[a]) for a in AXES}

    def member(group, offset):
        total = 1
        index = 0
        for a in group:
            total *= size_of[a]
            index = index * size_of[a] + here[a]
        target = lax.rem(index + offset, total)
        device = {}
        for a in reversed(group):
            device[a] = lax.rem(target, size_of[a])
            target = target // size_of[a]
        return {a: device.get(a, here[a]) for a in AXES}, index, total

    octant = [(1, 0, 0), (0, 1, 0), (1, 1, 0), (0, 0, 1), (1, 0, 1), (0, 1, 1), (1, 1, 1)]
    barrier = pltpu.get_barrier_semaphore()
    greeted = 0
    for group in groups:
        total = member(group, 0)[2]
        for offset in range(1, total):
            pl.semaphore_signal(
                barrier, inc=1, device_id=member(group, offset)[0], device_id_type=MESH
            )
            greeted += 1
    for dz, dy, dx in octant:
        for sign in (1, -1):
            pl.semaphore_signal(
                barrier, inc=1, device_id=neighbour(sign * dz, sign * dy, sign * dx),
                device_id_type=MESH,
            )
            greeted += 1

    def split_store(kind, cell, value):
        high = value.astype(BF16)
        low = (value - high.astype(F32)).astype(BF16)
        start = cell * 128 if isinstance(cell, int) else pl.multiple_of(cell * 128, 128)
        stack[kind * 32 : kind * 32 + 32, pl.ds(start, 128)] = jnp.concatenate([high, low], 0)

    @pl.loop(0, own)
    def _(cell):
        split_store(HX, cell, hx_ref[cell])
        split_store(HP, cell, hp_ref[cell])
        split_store(XX, cell, x_ref[cell])
        split_store(PP, cell, p_ref[cell])

    def products(left, right_from, right_to):
        m = lax.dot_general(
            stack[left * 32 : left * 32 + 32, :],
            stack[right_from * 32 : right_to * 32, :],
            (((1,), (1,)), ((), ())),
            preferred_element_type=F32,
        )
        return m[:cols] + m[cols:]

    def reduced(which, payload):
        base = which * sum(member(g, 0)[2] for g in groups)
        for phase, group in enumerate(groups):
            buf = bufs[which][phase]
            _, index, total = member(group, 0)
            buf[index] = payload
            if phase == 0 and which == 0:
                pl.semaphore_wait(barrier, greeted)
            copies = []
            for offset in range(1, total):
                copies.append(
                    pltpu.make_async_remote_copy(
                        src_ref=buf.at[index],
                        dst_ref=buf.at[index],
                        send_sem=red_send.at[base + offset],
                        recv_sem=red_recv.at[base + offset],
                        device_id=member(group, offset)[0],
                        device_id_type=MESH,
                    )
                )
                copies[-1].start()
            base += total
            yield None
            for copy in copies:
                copy.wait()
            payload = buf[0]
            for slot in range(1, total):
                payload = payload + buf[slot]
        yield payload

    def finish(steps):
        out = None
        for out in steps:
            pass
        return out

    x_row = products(XX, HX, WW)
    hx_row = products(HX, HX, WW)
    p_row = products(PP, HX, WW)
    first = jnp.where(lane < 32, pltpu.roll(hx_row, 64, 1), x_row)
    reduction = reduced(0, jnp.concatenate([first, p_row], 0))
    next(reduction)

    lane64 = lax.broadcasted_iota(jnp.int32, (BZ * BY * nproj, 128), 1)
    per_slot = BZ * BY * nproj
    for s in range(slots):
        ox = off_ref[2 * slots + s]
        rolled = pltpu.roll(beta_ref[s * per_slot : (s + 1) * per_slot, :], ox, 1)
        blo[s * per_slot : (s + 1) * per_slot, :] = jnp.where(lane64 >= ox, rolled, 0.0)
        bhi[s * per_slot : (s + 1) * per_slot, :] = jnp.where(lane64 < ox, rolled, 0.0)
    rim_y = BY + 2
    rim = (BZ + 2) * rim_y

    @pl.loop(0, slots * rim)
    def _(i):
        pieces[i] = jnp.zeros(pieces.shape[1:], F32)

    sums1 = finish(reduction)
    red1_ref[...] = sums1
    folded = sums1[:cols] + pltpu.roll(sums1[:cols], 112, 1)
    matrix = jnp.concatenate([pltpu.roll(folded, 64, 1), folded], 0)
    lane2 = lax.broadcasted_iota(jnp.int32, (2 * cols, 128), 1)
    matrix = jnp.where(lane2 < cols, matrix, 0.0)
    for k in range(cols):
        row = matrix[k : k + 1, :]
        column = matrix[:, k : k + 1] / matrix[k : k + 1, k : k + 1]
        matrix = jnp.where(lane2 == k, column, matrix - column * row)
    theta_t = matrix[cols:, :]
    theta_cols = [jnp.broadcast_to(theta_t[:, k : k + 1], (cols, 128)) for k in range(cols)]

    @pl.loop(0, own)
    def _(cell):
        xs = x_ref[cell]
        value = hx_ref[cell]
        for k in range(cols):
            value = value - theta_cols[k] * xs[k : k + 1, :]
        vv = v_ref[cell]
        value = value / (1.0 + vv * vv)
        zext[own + cell] = value
        w_ref[cell] = value
        split_store(WW, cell, value)

    for q in range(tiles_of(own)):
        low = jnp.zeros((cols, 128), F32)
        high = low
        for j in range(min(8, own - 8 * q)):
            tile = zext[own + 8 * q + j]
            keep = (lane >= 16 * j) & (lane < 16 * j + 16)
            low = jnp.where(keep, pltpu.roll(tile, 16 * j, 1) if j else tile, low)
            high = jnp.where(keep, pltpu.roll(tile, (16 * j + 16) % 128, 1) if j < 7 else tile, high)
        plow[q] = low
        phigh[q] = high

    two_y = ny == 2
    mine = zext.at[pl.ds(own, own)]
    sends = [
        (mine, ybuf.at[1], (0, -1, 0)),
        (mine, zext.at[pl.ds(2 * own, own)], (-1, 0, 0)),
        (mine, zext.at[pl.ds(0, own)], (1, 0, 0)),
    ]
    if not two_y:
        sends.append((mine, ybuf.at[0], (0, 1, 0)))
    sends += [
        (plow, xr.at[0], (0, 0, -1)),
        (phigh, xl, (0, 0, 1)),
        (plow, xr.at[1], (-1, 0, -1)),
        (plow, xr.at[2], (0, -1, -1)),
        (plow, xr.at[3], (-1, -1, -1)),
        (zext.at[pl.ds(own, (BZ - 1) * cy)], zybuf, (-1, -1, 0)),
    ]

    def launch(sends, send_sem, recv_sem):
        copies = []
        for i, (source, target, where) in enumerate(sends):
            copies.append(
                pltpu.make_async_remote_copy(
                    src_ref=source,
                    dst_ref=target,
                    send_sem=send_sem.at[i],
                    recv_sem=recv_sem.at[i],
                    device_id=neighbour(*where),
                    device_id_type=MESH,
                )
            )
            copies[-1].start()
        return copies

    copies = launch(sends, halo_send, halo_recv)
    w_row = products(WW, HX, WW)
    w_row2 = products(WW, XX, HW)
    for copy in copies:
        copy.wait()

    below_y = 1 if two_y else 0
    for z in range(fz):
        for y in range(fy):
            up_z, up_y = z >= cz, y >= cy
            local = (z - cz * up_z) * cy + (y - cy * up_y)
            if up_z and up_y:
                tile = zybuf[local]
            elif up_z:
                tile = zext[2 * own + local]
            elif up_y:
                tile = ybuf[1, local]
            else:
                tile = zext[own + local]
            frame[z * fy + y] = tile
            shift = (128 - 16 * (local % 8)) % 128
            tile = xr[up_z + 2 * up_y, local // 8]
            tile = pltpu.roll(tile, shift, 1) if shift else tile
            frame_x[z * fy + y] = tile
            if not up_z and not up_y:
                left = xl[local // 8]
                turn = (112 - 16 * (local % 8)) % 128
                left = pltpu.roll(left, turn, 1) if turn else left
                halo_x[local] = jnp.where(lane < 64, tile, left)

    @pl.loop(0, slots)
    def _(s):
        oz, oy = off_ref[s], off_ref[slots + s]
        sums = [jnp.zeros((cols, 128), F32) for _ in range(nproj)]
        for a in range(BZ):
            for b in range(BY):
                at = (oz + a) * fy + oy + b
                tile, tile_x = frame[at], frame_x[at]
                base = s * per_slot + (a * BY + b) * nproj
                for q in range(nproj):
                    sums[q] = sums[q] + tile * blo[pl.ds(base + q, 1), :]
                    sums[q] = sums[q] + jnp.where(
                        lane < 16, tile_x * bhi[pl.ds(base + q, 1), :], 0.0
                    )
        overlaps = [jnp.broadcast_to(jnp.sum(v, axis=1, keepdims=True), (cols, 128)) for v in sums]
        outs = []
        for p in range(nproj):
            value = overlaps[0] * d_ref[(s * nproj + p) * nproj]
            for q in range(1, nproj):
                value = value + overlaps[q] * d_ref[(s * nproj + p) * nproj + q]
            outs.append(value)
        for a in range(BZ):
            for b in range(BY):
                base = s * per_slot + (a * BY + b) * nproj
                low = outs[0] * blo[pl.ds(base, 1), :]
                high = outs[0] * bhi[pl.ds(base, 1), :]
                for p in range(1, nproj):
                    low = low + outs[p] * blo[pl.ds(base + p, 1), :]
                    high = high + outs[p] * bhi[pl.ds(base + p, 1), :]
                place = s * rim + (a + 1) * rim_y + b + 1
                pieces[place, 0] = low
                pieces[place, 1] = high

    @pl.loop(0, fz)
    def _(z):
        starts = []
        for s in range(slots):
            a = jnp.minimum(jnp.maximum(z - off_ref[s], -1), BZ) + 1
            starts.append(s * rim + a * rim_y)
        for y in range(fy):
            low = jnp.zeros((cols, 128), F32)
            high = low
            for s in range(slots):
                b = jnp.minimum(jnp.maximum(y - off_ref[slots + s], -1), BY) + 1
                low = low + pieces[starts[s] + b, 0]
                high = high + pieces[starts[s] + b, 1]
            nf[z, y] = low
            nh[z, y] = high

    spans = []
    filled = 0
    for up_z in (0, 1):
        for up_y in (0, 1):
            cells = [
                (z, y)
                for z in (range(cz, fz) if up_z else range(cz))
                for y in (range(cy, fy) if up_y else range(cy))
            ]
            spans.append((filled, up_z, up_y, cells))
            for q in range(tiles_of(len(cells))):
                tile = jnp.zeros((cols, 128), F32)
                for j, (z, y) in enumerate(cells[8 * q : 8 * q + 8]):
                    keep = (lane >= 16 * j) & (lane < 16 * j + 16)
                    value = nh[z, y]
                    tile = jnp.where(keep, pltpu.roll(value, 16 * j, 1) if j else value, tile)
                spack[filled + q] = tile
            filled += tiles_of(len(cells))
    more_z, more_y = fz - cz, fy - cy
    sends = [
        (nf.at[pl.ds(cz, more_z), pl.ds(0, cy)], rz, (1, 0, 0)),
        (nf.at[pl.ds(0, cz), pl.ds(cy, more_y)], ry, (0, 1, 0)),
        (nf.at[pl.ds(cz, more_z), pl.ds(cy, more_y)], rzy, (1, 1, 0)),
    ]
    for begin, up_z, up_y, cells in spans:
        part = pl.ds(begin, tiles_of(len(cells)))
        sends.append((spack.at[part], rx.at[part], (up_z, up_y, 1)))
    copies = launch(sends, spill_send, spill_recv)

    @pl.loop(0, cz)
    def _(z):
        for y in range(cy):
            cell = z * cy + y
            centre = zext[own + cell]
            edge = halo_x[cell]
            vv = v_ref[cell]
            total = centre * (vv - 1.5 * LAP_CENTER)
            for k, weight in enumerate(LAP_COEFFS, start=1):
                beside = zext[own + cell + k * cy] + zext[own + cell - k * cy]
                for target in (y + k, y - k):
                    if target >= cy:
                        beside = beside + ybuf[1, z * cy + target - cy]
                    elif target < 0:
                        beside = beside + ybuf[below_y, z * cy + target + cy]
                    else:
                        beside = beside + zext[own + z * cy + target]
                beside = beside + pltpu.roll(jnp.where(lane < k, edge, centre), 128 - k, 1)
                beside = beside + pltpu.roll(jnp.where(lane >= 128 - k, edge, centre), k, 1)
                total = total - 0.5 * weight * beside
            hw_ref[cell] = total + nf[z, y]

    for copy in copies:
        copy.wait()
    for z in range(cz):
        for y in range(cy):
            cell = z * cy + y
            value = hw_ref[cell]
            if z < more_z:
                value = value + rz[z, y]
            if y < more_y:
                value = value + ry[z, y]
            if z < more_z and y < more_y:
                value = value + rzy[z, y]
            extra = None
            for begin, up_z, up_y, cells in spans:
                where = (z + cz * up_z, y + cy * up_y)
                if where in cells:
                    index = cells.index(where)
                    tile = rx[begin + index // 8]
                    shift = (128 - 16 * (index % 8)) % 128
                    tile = pltpu.roll(tile, shift, 1) if shift else tile
                    extra = tile if extra is None else extra + tile
            value = value + jnp.where(lane < 16, extra, 0.0)
            hw_ref[cell] = value
            split_store(HW, cell, value)

    hw_row = products(HW, XX, HW + 1)
    second = jnp.where(lane < 96, hw_row, pltpu.roll(w_row2_pad(w_row2), 32, 1))
    red2_ref[...] = finish(reduced(1, jnp.concatenate([w_row, second], 0)))


def w_row2_pad(row):
    return jnp.concatenate([row, jnp.zeros((row.shape[0], 128 - row.shape[1]), row.dtype)], 1)


def per_device(
    sizes,
    block_x, block_hx, block_p, block_hp, potential, projectors, coupling,
    atom_count, proj_count, offsets, extents,
):
    cols, cz, cy, cx = block_x.shape
    slots, nproj = projectors.shape[-3], projectors.shape[-2]
    nz, ny, nx = sizes
    own = cz * cy
    fz, fy = cz + BZ - 1, cy + BY - 1
    beta = masked_projectors(projectors, atom_count, proj_count, extents)[0, 0, 0]
    beta = beta.reshape(slots, nproj, BZ * BY, BX).transpose(0, 2, 1, 3)
    beta = beta.reshape(slots * BZ * BY * nproj, BX)
    beta = jnp.pad(beta, ((0, 0), (0, 128 - BX)))
    sym = (0.5 * (coupling + jnp.swapaxes(coupling, -1, -2))).reshape(-1)
    turned = [
        jnp.transpose(b, (1, 2, 0, 3)).reshape(own, cols, cx)
        for b in (block_x, block_hx, block_p, block_hp)
    ]
    groups = (("gz", "gy"), ("gx",)) if nz * ny <= 16 else (("gz",), ("gy",), ("gx",))
    size_of = dict(zip(AXES, sizes))
    totals = []
    for group in groups:
        total = 1
        for a in group:
            total *= size_of[a]
        totals.append(total)
    tile = (cols, 128)
    more_z, more_y = fz - cz, fy - cy
    packed = sum(
        tiles_of(zc * yc) for zc in (cz, more_z) for yc in (cy, more_y)
    )
    per_slot = BZ * BY * nproj
    scratch = [
        pltpu.VMEM((192, own * 128), BF16),
        pltpu.VMEM((3 * own,) + tile, F32),
        pltpu.VMEM((2, own) + tile, F32),
        pltpu.VMEM(((BZ - 1) * cy,) + tile, F32),
        pltpu.VMEM((tiles_of(own),) + tile, F32),
        pltpu.VMEM((tiles_of(own),) + tile, F32),
        pltpu.VMEM((4, tiles_of(own)) + tile, F32),
        pltpu.VMEM((tiles_of(own),) + tile, F32),
        pltpu.VMEM((fz * fy,) + tile, F32),
        pltpu.VMEM((fz * fy,) + tile, F32),
        pltpu.VMEM((own,) + tile, F32),
        pltpu.VMEM((slots * per_slot, 128), F32),
        pltpu.VMEM((slots * per_slot, 128), F32),
        pltpu.VMEM((slots * (BZ + 2) * (BY + 2), 2) + tile, F32),
        pltpu.VMEM((fz, fy) + tile, F32),
        pltpu.VMEM((fz, fy) + tile, F32),
        pltpu.VMEM((packed,) + tile, F32),
        pltpu.VMEM((more_z, cy) + tile, F32),
        pltpu.VMEM((cz, more_y) + tile, F32),
        pltpu.VMEM((more_z, more_y) + tile, F32),
        pltpu.VMEM((packed,) + tile, F32),
        pltpu.VMEM((8, 128), F32),
    ]
    scratch += [pltpu.VMEM((t, 2 * cols, 128), F32) for t in totals] * 2
    scratch += [
        pltpu.SemaphoreType.DMA((2 * sum(totals),)),
        pltpu.SemaphoreType.DMA((2 * sum(totals),)),
        pltpu.SemaphoreType.DMA((10,)),
        pltpu.SemaphoreType.DMA((10,)),
        pltpu.SemaphoreType.DMA((7,)),
        pltpu.SemaphoreType.DMA((7,)),
    ]
    vmem = pl.BlockSpec(memory_space=pltpu.VMEM)
    smem = pl.BlockSpec(memory_space=pltpu.SMEM)
    w, hw, red1, red2 = pl.pallas_call(
        functools.partial(kernel, sizes, groups, (cz, cy, cx, slots, nproj, cols)),
        out_shape=(
            jax.ShapeDtypeStruct((own,) + tile, F32),
            jax.ShapeDtypeStruct((own,) + tile, F32),
            jax.ShapeDtypeStruct((2 * cols, 128), F32),
            jax.ShapeDtypeStruct((2 * cols, 128), F32),
        ),
        in_specs=[smem, smem] + [vmem] * 6,
        out_specs=(vmem,) * 4,
        scratch_shapes=scratch,
        compiler_params=pltpu.CompilerParams(collective_id=0, has_side_effects=True),
    )(offsets.reshape(-1), sym, *turned, potential.reshape(own, 1, cx), beta)
    weight = 1.0 / (own * cx * nz * ny * nx)

    def block(rows, group):
        start = 32 * group
        return (rows[:, start : start + cols] + rows[:, start + cols : start + 2 * cols]) * weight

    x_row, p_row, w_row, hw_row = red1[:cols], red1[cols:], red2[:cols], red2[cols:]
    gram = jnp.block(
        [
            [block(x_row, 2), block(w_row, 2).T, block(x_row, 3)],
            [block(w_row, 2), block(hw_row, 3), block(w_row, 3)],
            [block(p_row, 2), block(w_row, 3).T, block(p_row, 3)],
        ]
    )
    rayleigh = jnp.block(
        [
            [block(x_row, 0).T, block(hw_row, 0).T, block(x_row, 1)],
            [block(w_row, 0), block(hw_row, 2).T, block(w_row, 1)],
            [block(p_row, 0), block(hw_row, 1).T, block(p_row, 1)],
        ]
    )
    w, hw = (jnp.transpose(b.reshape(cz, cy, cols, cx), (2, 0, 1, 3)) for b in (w, hw))
    return (w, hw, gram, rayleigh)


def solution(mesh):
    sizes = tuple(mesh.shape[a] for a in AXES)
    in_specs = (
        P(None, "gz", "gy", "gx"),
        P(None, "gz", "gy", "gx"),
        P(None, "gz", "gy", "gx"),
        P(None, "gz", "gy", "gx"),
        P("gz", "gy", "gx"),
        P("gz", "gy", "gx", None, None, None),
        P("gz", "gy", "gx", None, None, None),
        P("gz", "gy", "gx"),
        P("gz", "gy", "gx", None),
        P(None, "gz", "gy", "gx", None),
        P(None, "gz", "gy", "gx", None),
    )
    out_specs = (P(None, "gz", "gy", "gx"), P(None, "gz", "gy", "gx"), P(), P())
    return jax.shard_map(
        functools.partial(per_device, sizes),
        mesh=mesh, in_specs=in_specs, out_specs=out_specs, check_vma=False,
    )
```

time: 324 us -> 64.9 us (0.20)
  waiting for transfers between devices: 86.4 us -> 0 us
  blocking collectives: 82.9 us -> 0 us
  local copies, waits for them, and re-layouts: 62 us -> 8.37 us
  Pallas kernels: 0 us -> 51.7 us
  loops' own time: 45.6 us -> 0 us
  starting transfers between devices: 16.1 us -> 0 us
  other arithmetic: 18.4 us -> 2.88 us
  matrix products: 9.65 us -> 0 us
    ppermute x12 -> x0, waiting for transfers between devices: 86.4 us -> none  [the longest x6 80.5 us: shifted(): return lax.ppermute(value, axis, pairs)]
    psum x2 -> x0, blocking collectives: 82.9 us -> none  [the longest x1 42.1 us: per_device(): lax.psum((inner_product(block_x, block_x), inner_product(block_x, block_h...]
    pallas_call x0 -> x1, Pallas kernels: none -> 51.7 us  [per_device(): pl.pallas_call(functools.partial(kernel, sizes, groups, (cz, cy, cx, slot...]
    another operation x2 -> x0, loops' own time: 45.6 us -> none  [the longest x1 45.5 us: deposit_boxes(): return lax.fori_loop(0, corners.shape[0], add_single, frame_block)]
    gather x32 -> x0, local copies, waits for them, and re-layouts: 26.7 us -> none
    dynamic_update_slice x16 -> x0, local copies, waits for them, and re-layouts: 21.2 us -> none  [add_single(): return lax.dynamic_update_slice(current, updated, position)]
    ppermute x12 -> x0, starting transfers between devices: 16.1 us -> none  [the longest x6 10 us: shifted(): return lax.ppermute(value, axis, pairs)]
    add x13 -> x0, other arithmetic: 9.83 us -> none  [the longest x1 7.21 us: per_device(): hw_block = kinetic_part + potential * w_block + nonlocal_part]
  transfers between devices with their start and end apart: 12 -> 0, of which waited for: 6 -> 0; matrix products, arithmetic and copies ran while one was open for 21% -> 0% of each run, Pallas kernels for 0% -> 0%
where the time goes in v1:
time: 64.9 us; the launch traced here: 64.4 us
  Pallas kernels  51.7 us (80%)
  local copies, waits for them, and re-layouts  8.37 us (13%)
  other arithmetic  2.88 us (4%)
  between operations  1.38 us (2%)
    pallas_call x1, Pallas kernels, per_device(): pl.pallas_call(functools.partial(kernel, sizes, groups, (cz, cy, cx, slot...  51.7 us
    unnamed x22, local copies, waits for them, and re-layouts  4.94 us

profile of v1, /device:TPU:0, one launch (start us, length us, event | category | flops | bytes accessed | tf_op | source)
XLA Modules:
  0.0 64.4 jit_solution(13070969430129722511)
XLA Ops:
  1.3 0.6 %copy-done.9 = s32[1,1,1,8]{3,2,1,0:T(1,128)S(1)} copy-done((s32[1,1,1,8]{3,2,1,0:T(1,128)S(1)}, s32[1,1,1,8]{3,2,1,0:T(1,128)}, u32[]{:S(2)}) %copy-start.9) | copy-done | bytes 56
  1.9 0.1 fusion.2
  2.0 0.6 copy-done.7
  2.6 0.7 %copy-done.8 = s32[3,1,1,1,8]{4,3,2,1,0:T(1,128)S(1)} copy-done((s32[3,1,1,1,8]{4,3,2,1,0:T(1,128)S(1)}, s32[3,1,1,1,8]{4,3,2,1,0:T(1,128)}, u32[]{:S(2)}) %copy-start.8) | copy-done | bytes 120
  3.3 0.6 reshape.266.off_ref
  3.9 0.1 compare_and_fusion
  4.0 0.0 copy-done.6
  4.0 0.1 copy.86
  4.1 0.6 reshape.267.d_ref
  4.8 0.0 copy-done.5
  4.8 0.6 reshape.272.v_ref
  5.4 0.1 and_select_fusion
  5.5 0.1 reshape_squeeze.3
  5.6 0.1 copy.87
  5.7 0.7 %pad.4.beta_ref = f32[512,128]{1,0:T(8,128)} pad(f32[512,16]{1,0:T(8,128)S(1)} %bitcast.45, f32[]{:T(128)} %constant.60.clone.1), padding=0_0x0_112 | pad | bytes 294916 | tf_op jit(solution)/shard_map/jit(_pad)/pad | solution.py:424
  6.5 51.7 %shard_map.138 = (f32[36,16,128]{2,1,0:T(8,128)}, f32[36,16,128]{2,1,0:T(8,128)}, f32[32,128]{1,0:T(8,128)}, f32[32,128]{1,0:T(8,128)}) custom-call(s32[24]{0:T(128)} %reshape.266.off_ref, f32[128]{0:T(128)} %reshape.267.d_ref, f32[36,16,128]{2,1,0:T(8,128)} %bitcast.46, f32[36,16,128]{2,1,0:T(8,128)} %bitcast.47, f32[36,16,128]{2,1,0:T(8,128)} %bitcast.48, ...), custom_call_target="tpu_custom_call" | custom-call | tf_op jit(solution)/shard_map/pallas_call | solution.py:479
  58.2 1.1 %multiply_bitcast_fusion.2 = (f32[16,16]{0,1:T(8,128)S(1)}, f32[16,16]{1,0:T(8,128)S(1)}, f32[16,16]{1,0:T(8,128)S(1)}, f32[16,16]{1,0:T(8,128)S(1)}, f32[16,16]...) fusion(f32[32,128]{1,0:T(8,128)} %get-tuple-element.11), kind=kLoop, calls=%fused_computation.14 | loop fusion | flops 3584 | bytes 21504 | tf_op jit(solution)/shard_map/transpose | solution.py:508
  59.3 0.1 copy.94
  59.4 0.1 copy.95
  59.5 0.1 copy.96
  59.6 0.1 copy.92
  59.6 0.6 copy-done.1
  60.2 0.1 copy.88
  60.3 0.1 copy.91
  60.4 0.6 copy-done
  61.0 0.1 multiply_bitcast_fusion.3
  61.1 0.7 %maximum_maximum_fusion = f32[48,48]{1,0:T(8,128)} fusion(f32[16,16]{1,0:T(8,128)S(1)} %get-tuple-element.21, f32[16,16]{1,0:T(8,128)S(1)} %copy.92, f32[16,16]{1,0:T(8,128)S(1)} %get-tuple-element.23, f32[16,16]{1,0:T(8,128)S(1)} %get-tuple-element.30, f32[16,16]{1,0:T(8,128)S(1)} %get-tuple-element.32, f32[16,16]{1,0:T(8,128)S(1)} %copy.91, ...), kind=kLoop, calls=%fused_computation.1 | loop fusion | flops 18432 | bytes 18432 | tf_op jit(solution)/shard_map/jit(block)/concatenate | solution.py:499
  61.8 0.1 copy.93
  61.9 0.7 %maximum_maximum_fusion.1 = f32[48,48]{1,0:T(8,128)} fusion(f32[16,16]{1,0:T(8,128)S(1)} %get-tuple-element.27, f32[16,16]{1,0:T(8,128)S(1)} %copy.96, f32[16,16]{1,0:T(8,128)S(1)} %get-tuple-element.24, f32[16,16]{1,0:T(8,128)S(1)} %get-tuple-element.29, f32[16,16]{1,0:T(8,128)S(1)} %copy.95, f32[16,16]{1,0:T(8,128)S(1)} %get-tuple-element.31, ...), kind=kLoop, calls=%fused_computation.2 | loop fusion | flops 18432 | bytes 18432 | tf_op jit(solution)/shard_map/jit(block)/concatenate | solution.py:506
  62.6 0.7 %copy.101 = f32[16,6,6,128]{3,0,2,1:T(8,128)} copy(f32[16,6,6,128]{3,0,2,1:T(8,128)S(1)} %bitcast.51) | data formatting | bytes 589824
  63.3 0.4 copy-done.2
  63.7 0.7 %copy.102 = f32[16,6,6,128]{3,0,2,1:T(8,128)} copy(f32[16,6,6,128]{3,0,2,1:T(8,128)S(1)} %bitcast.50) | data formatting | bytes 589824
  (20 shorter events, 0.1 us)
Async XLA Ops:
  1.3 0.7 %copy-start.9 = (s32[1,1,1,8]{3,2,1,0:T(1,128)S(1)}, s32[1,1,1,8]{3,2,1,0:T(1,128)}, u32[]{:S(2)}) copy-start(s32[1,1,1,8]{3,2,1,0:T(1,128)} %param.19) | copy-start | bytes 100
  1.9 0.7 %copy-start.7 = (s32[3,1,1,1,8]{4,3,2,1,0:T(1,128)S(1)}, s32[3,1,1,1,8]{4,3,2,1,0:T(1,128)}, u32[]{:S(2)}) copy-start(s32[3,1,1,1,8]{4,3,2,1,0:T(1,128)} %param.21) | copy-start | bytes 292
  2.6 0.7 %copy-start.8 = (s32[3,1,1,1,8]{4,3,2,1,0:T(1,128)S(1)}, s32[3,1,1,1,8]{4,3,2,1,0:T(1,128)}, u32[]{:S(2)}) copy-start(s32[3,1,1,1,8]{4,3,2,1,0:T(1,128)} %param.20) | copy-start | bytes 292
  3.3 0.7 %copy-start.6 = (f32[1,1,1,8,4,4]{3,5,4,2,1,0:T(4,128)S(1)}, f32[1,1,1,8,4,4]{3,5,4,2,1,0:T(4,128)}, u32[]{:S(2)}) copy-start(f32[1,1,1,8,4,4]{3,5,4,2,1,0:T(4,128)} %param.17) | copy-start | bytes 1540
  4.0 0.7 %copy-start.5 = (f32[6,6,128]{2,1,0:T(8,128)S(1)}, f32[6,6,128]{2,1,0:T(8,128)}, u32[]{:S(2)}) copy-start(f32[6,6,128]{2,1,0:T(8,128)} %param.15) | copy-start | bytes 55300
  4.1 1.3 %copy-start.4 = (f32[1,1,1,8,4,256]{5,4,3,2,1,0:T(4,128)S(1)}, f32[1,1,1,8,4,256]{5,4,3,2,1,0:T(4,128)}, u32[]{:S(2)}) copy-start(f32[1,1,1,8,4,256]{5,4,3,2,1,0:T(4,128)} %param.16) | copy-start | bytes 98308
  59.5 0.7 %copy-start.1 = (f32[32,128]{1,0:T(8,128)S(1)}, f32[32,128]{1,0:T(8,128)}, u32[]{:S(2)}) copy-start(f32[32,128]{1,0:T(8,128)} %get-tuple-element.11) | copy-start | bytes 49156
  60.3 0.7 %copy-start = (f32[32,128]{1,0:T(8,128)S(1)}, f32[32,128]{1,0:T(8,128)}, u32[]{:S(2)}) copy-start(f32[32,128]{1,0:T(8,128)} %get-tuple-element.10) | copy-start | bytes 49156
  60.3 2.3 %copy-start.3 = (f32[36,16,128]{2,1,0:T(8,128)S(1)}, f32[36,16,128]{2,1,0:T(8,128)}, u32[]{:S(2)}) copy-start(f32[36,16,128]{2,1,0:T(8,128)} %get-tuple-element.8) | copy-start | bytes 884740
  62.6 1.1 %copy-start.2 = (f32[36,16,128]{2,1,0:T(8,128)S(1)}, f32[36,16,128]{2,1,0:T(8,128)}, u32[]{:S(2)}) copy-start(f32[36,16,128]{2,1,0:T(8,128)} %get-tuple-element.9) | copy-start | bytes 884740

commit v2 on v1

--- a/solution.py
+++ b/solution.py
@@ -14,25 +14,7 @@
 AXES = ("gz", "gy", "gx")
 F32 = jnp.float32
 BF16 = jnp.bfloat16
-HX, HP, XX, PP, WW, HW = range(6)
-
-
-def masked_projectors(projectors, atom_count, proj_count, extents):
-    slot_index = jnp.arange(projectors.shape[-3], dtype=jnp.int32)
-    live_slot = slot_index < atom_count[..., None]
-    proj_index = jnp.arange(projectors.shape[-2], dtype=jnp.int32)
-    live_proj = proj_index < proj_count[..., None]
-    cell_index = jnp.arange(projectors.shape[-1], dtype=jnp.int32)
-    along_z = cell_index // (BY * BX)
-    along_y = cell_index // BX % BY
-    along_x = cell_index % BX
-    inside = (
-        (along_z < extents[0][..., None])
-        & (along_y < extents[1][..., None])
-        & (along_x < extents[2][..., None])
-    )
-    keeper = live_slot[..., None, None] & live_proj[..., None] & inside[..., None, :]
-    return jnp.where(keeper, projectors, jnp.zeros_like(projectors))
+HP, HX, XX, PP, WW, HW = range(6)
 
 
 def tiles_of(count):
@@ -41,8 +23,8 @@
 
 def kernel(
     sizes, groups, dims,
-    off_ref, d_ref, x_ref, hx_ref, p_ref, hp_ref, v_ref, beta_ref,
-    w_ref, hw_ref, red1_ref, red2_ref,
+    off_ref, ext_ref, count_ref, proj_ref, d_ref, x_ref, hx_ref, p_ref, hp_ref, v_ref, beta_ref,
+    w_ref, hw_ref, gram_ref, ray_ref, red1_ref,
     stack, zext, ybuf, zybuf, plow, phigh, xr, xl, frame, frame_x, halo_x,
     blo, bhi, pieces, nf, nh, spack, rz, ry, rzy, rx, wout,
     *rest,
@@ -101,21 +83,24 @@
         start = cell * 128 if isinstance(cell, int) else pl.multiple_of(cell * 128, 128)
         stack[kind * 32 : kind * 32 + 32, pl.ds(start, 128)] = jnp.concatenate([high, low], 0)
 
-    @pl.loop(0, own)
-    def _(cell):
-        split_store(HX, cell, hx_ref[cell])
-        split_store(HP, cell, hp_ref[cell])
-        split_store(XX, cell, x_ref[cell])
-        split_store(PP, cell, p_ref[cell])
-
-    def products(left, right_from, right_to):
+    @pl.loop(0, cz)
+    def _(z):
+        for y in range(cy):
+            cell = z * cy + y
+            split_store(HX, cell, hx_ref[cell])
+            split_store(HP, cell, hp_ref[cell])
+            split_store(XX, cell, x_ref[cell])
+            split_store(PP, cell, p_ref[cell])
+
+    def products(left, right_from, right_to, count=1):
         m = lax.dot_general(
-            stack[left * 32 : left * 32 + 32, :],
+            stack[left * 32 : (left + count) * 32, :],
             stack[right_from * 32 : right_to * 32, :],
             (((1,), (1,)), ((), ())),
             preferred_element_type=F32,
         )
-        return m[:cols] + m[cols:]
+        parts = [m[32 * i : 32 * i + cols] + m[32 * i + cols : 32 * i + 32] for i in range(count)]
+        return parts if count > 1 else parts[0]
 
     def reduced(which, payload):
         base = which * sum(member(g, 0)[2] for g in groups)
@@ -153,31 +138,50 @@
             pass
         return out
 
-    x_row = products(XX, HX, WW)
-    hx_row = products(HX, HX, WW)
-    p_row = products(PP, HX, WW)
-    first = jnp.where(lane < 32, pltpu.roll(hx_row, 64, 1), x_row)
-    reduction = reduced(0, jnp.concatenate([first, p_row], 0))
+    hx_row, x_row, p_row = products(HX, HP, WW, 3)
+    first = jnp.where((lane >= 32) & (lane < 64), pltpu.roll(hx_row, 96, 1), x_row)
+
+    def paired(upper, lower):
+        upper = upper + pltpu.roll(upper, 112, 1)
+        lower = lower + pltpu.roll(lower, 112, 1)
+        return jnp.where(lane % 32 < 16, upper, pltpu.roll(lower, 16, 1))
+
+    reduction = reduced(0, paired(first, p_row))
     next(reduction)
 
-    lane64 = lax.broadcasted_iota(jnp.int32, (BZ * BY * nproj, 128), 1)
     per_slot = BZ * BY * nproj
+    lane_p = lax.broadcasted_iota(jnp.int32, (nproj, 128), 1)
+    row_p = lax.broadcasted_iota(jnp.int32, (nproj, 128), 0)
+    in_tile = 128 // BX
     for s in range(slots):
-        ox = off_ref[2 * slots + s]
-        rolled = pltpu.roll(beta_ref[s * per_slot : (s + 1) * per_slot, :], ox, 1)
-        blo[s * per_slot : (s + 1) * per_slot, :] = jnp.where(lane64 >= ox, rolled, 0.0)
-        bhi[s * per_slot : (s + 1) * per_slot, :] = jnp.where(lane64 < ox, rolled, 0.0)
+        ox = off_ref[2, s]
+        along = lax.rem(lane_p - ox + 128, 128)
+        along = jnp.where(row_p < proj_ref[0, s], along, 128)
+        low_side = lane_p >= ox
+        live = s < count_ref[0, 0]
+        for a in range(BZ):
+            for b in range(BY):
+                used = live & (a < ext_ref[0, s]) & (b < ext_ref[1, s])
+                limit = jnp.where(used, jnp.minimum(ext_ref[2, s], BX), 0)
+                box = a * BY + b
+                part = beta_ref[s, :, (box // in_tile) * 128 : (box // in_tile) * 128 + 128]
+                part = pltpu.roll(part, lax.rem(ox + 128 - BX * (box % in_tile), 128), 1)
+                part = jnp.where(along < limit, part, 0.0)
+                row = s * per_slot + box * nproj
+                blo[row : row + nproj, :] = jnp.where(low_side, part, 0.0)
+                bhi[row : row + nproj, :] = jnp.where(low_side, 0.0, part)
     rim_y = BY + 2
     rim = (BZ + 2) * rim_y
 
-    @pl.loop(0, slots * rim)
-    def _(i):
-        pieces[i] = jnp.zeros(pieces.shape[1:], F32)
+    @pl.loop(0, slots)
+    def _(s):
+        for i in range(rim):
+            if i < rim_y or i >= rim - rim_y or i % rim_y in (0, rim_y - 1):
+                pieces[s * rim + i] = jnp.zeros(pieces.shape[1:], F32)
 
     sums1 = finish(reduction)
     red1_ref[...] = sums1
-    folded = sums1[:cols] + pltpu.roll(sums1[:cols], 112, 1)
-    matrix = jnp.concatenate([pltpu.roll(folded, 64, 1), folded], 0)
+    matrix = jnp.concatenate([pltpu.roll(sums1, 64, 1), pltpu.roll(sums1, 96, 1)], 0)
     lane2 = lax.broadcasted_iota(jnp.int32, (2 * cols, 128), 1)
     matrix = jnp.where(lane2 < cols, matrix, 0.0)
     for k in range(cols):
@@ -187,23 +191,25 @@
     theta_t = matrix[cols:, :]
     theta_cols = [jnp.broadcast_to(theta_t[:, k : k + 1], (cols, 128)) for k in range(cols)]
 
-    @pl.loop(0, own)
-    def _(cell):
-        xs = x_ref[cell]
-        value = hx_ref[cell]
-        for k in range(cols):
-            value = value - theta_cols[k] * xs[k : k + 1, :]
-        vv = v_ref[cell]
-        value = value / (1.0 + vv * vv)
-        zext[own + cell] = value
-        w_ref[cell] = value
-        split_store(WW, cell, value)
+    @pl.loop(0, cz)
+    def _(z):
+        for y in range(cy):
+            cell = z * cy + y
+            xs = x_ref[cell]
+            value = hx_ref[cell]
+            for k in range(cols):
+                value = value - theta_cols[k] * xs[k : k + 1, :]
+            vv = v_ref[z, y : y + 1, :]
+            value = value / (1.0 + vv * vv)
+            zext[cz + z, y] = value
+            w_ref[cell] = value
+            split_store(WW, cell, value)
 
     for q in range(tiles_of(own)):
         low = jnp.zeros((cols, 128), F32)
         high = low
         for j in range(min(8, own - 8 * q)):
-            tile = zext[own + 8 * q + j]
+            tile = zext[cz + (8 * q + j) // cy, (8 * q + j) % cy]
             keep = (lane >= 16 * j) & (lane < 16 * j + 16)
             low = jnp.where(keep, pltpu.roll(tile, 16 * j, 1) if j else tile, low)
             high = jnp.where(keep, pltpu.roll(tile, (16 * j + 16) % 128, 1) if j < 7 else tile, high)
@@ -211,26 +217,37 @@
         phigh[q] = high
 
     two_y = ny == 2
-    mine = zext.at[pl.ds(own, own)]
-    sends = [
-        (mine, ybuf.at[1], (0, -1, 0)),
-        (mine, zext.at[pl.ds(2 * own, own)], (-1, 0, 0)),
-        (mine, zext.at[pl.ds(0, own)], (1, 0, 0)),
+    more_z, more_y = fz - cz, fy - cy
+    z_tiles = tiles_of(more_z * cy)
+    corner_tiles = tiles_of((more_z - 1) * cy + more_y)
+
+    def some(ref, z, dz, y, dy):
+        return ref.at[pl.ds(z, dz), pl.ds(y, dy)]
+
+    def layers(target, base, z, dz, y, dy, where):
+        return some(zext, cz + z, dz, y, dy), some(target, base + z, dz, y, dy), where
+
+    early = [
+        (some(zext, cz, more_z, 0, more_y), zybuf, (-1, -1, 0)),
+        (plow.at[pl.ds(0, corner_tiles)], xr.at[3, pl.ds(0, corner_tiles)], (-1, -1, -1)),
+        (plow, xr.at[2], (0, -1, -1)),
+        (plow.at[pl.ds(0, z_tiles)], xr.at[1, pl.ds(0, z_tiles)], (-1, 0, -1)),
+        (plow, xr.at[0], (0, 0, -1)),
+        layers(ybuf.at[1], 0, 0, cz, 0, more_y, (0, -1, 0)),
+        layers(zext, 2 * cz, 0, more_z, 0, cy, (-1, 0, 0)),
+    ]
+    late = [
+        (phigh, xl, (0, 0, 1)),
+        layers(ybuf.at[1], 0, 0, cz, more_y, cy - more_y, (0, -1, 0)),
+        layers(zext, 2 * cz, more_z, cz - more_z, 0, cy, (-1, 0, 0)),
+        layers(zext, 0, 0, cz, 0, cy, (1, 0, 0)),
     ]
     if not two_y:
-        sends.append((mine, ybuf.at[0], (0, 1, 0)))
-    sends += [
-        (plow, xr.at[0], (0, 0, -1)),
-        (phigh, xl, (0, 0, 1)),
-        (plow, xr.at[1], (-1, 0, -1)),
-        (plow, xr.at[2], (0, -1, -1)),
-        (plow, xr.at[3], (-1, -1, -1)),
-        (zext.at[pl.ds(own, (BZ - 1) * cy)], zybuf, (-1, -1, 0)),
-    ]
-
-    def launch(sends, send_sem, recv_sem):
+        late.append(layers(ybuf.at[0], 0, 0, cz, 0, cy, (0, 1, 0)))
+
+    def launch(sends, send_sem, recv_sem, first=0):
         copies = []
-        for i, (source, target, where) in enumerate(sends):
+        for i, (source, target, where) in enumerate(sends, start=first):
             copies.append(
                 pltpu.make_async_remote_copy(
                     src_ref=source,
@@ -244,8 +261,9 @@
             copies[-1].start()
         return copies
 
-    copies = launch(sends, halo_send, halo_recv)
-    w_row = products(WW, HX, WW)
+    copies = launch(early, halo_send, halo_recv)
+    late_copies = launch(late, halo_send, halo_recv, len(early))
+    w_row = products(WW, HP, WW)
     w_row2 = products(WW, XX, HW)
     for copy in copies:
         copy.wait()
@@ -256,27 +274,22 @@
             up_z, up_y = z >= cz, y >= cy
             local = (z - cz * up_z) * cy + (y - cy * up_y)
             if up_z and up_y:
-                tile = zybuf[local]
+                tile = zybuf[z - cz, y - cy]
             elif up_z:
-                tile = zext[2 * own + local]
+                tile = zext[cz + z, y]
             elif up_y:
-                tile = ybuf[1, local]
+                tile = ybuf[1, z, y - cy]
             else:
-                tile = zext[own + local]
+                tile = zext[cz + z, y]
             frame[z * fy + y] = tile
             shift = (128 - 16 * (local % 8)) % 128
             tile = xr[up_z + 2 * up_y, local // 8]
             tile = pltpu.roll(tile, shift, 1) if shift else tile
             frame_x[z * fy + y] = tile
-            if not up_z and not up_y:
-                left = xl[local // 8]
-                turn = (112 - 16 * (local % 8)) % 128
-                left = pltpu.roll(left, turn, 1) if turn else left
-                halo_x[local] = jnp.where(lane < 64, tile, left)
 
     @pl.loop(0, slots)
     def _(s):
-        oz, oy = off_ref[s], off_ref[slots + s]
+        oz, oy = off_ref[0, s], off_ref[1, s]
         sums = [jnp.zeros((cols, 128), F32) for _ in range(nproj)]
         for a in range(BZ):
             for b in range(BY):
@@ -291,9 +304,10 @@
         overlaps = [jnp.broadcast_to(jnp.sum(v, axis=1, keepdims=True), (cols, 128)) for v in sums]
         outs = []
         for p in range(nproj):
-            value = overlaps[0] * d_ref[(s * nproj + p) * nproj]
-            for q in range(1, nproj):
-                value = value + overlaps[q] * d_ref[(s * nproj + p) * nproj + q]
+            value = overlaps[p] * d_ref[s, p, p]
+            for q in range(nproj):
+                if q != p:
+                    value = value + overlaps[q] * (0.5 * (d_ref[s, p, q] + d_ref[s, q, p]))
             outs.append(value)
         for a in range(BZ):
             for b in range(BY):
@@ -311,13 +325,13 @@
     def _(z):
         starts = []
         for s in range(slots):
-            a = jnp.minimum(jnp.maximum(z - off_ref[s], -1), BZ) + 1
+            a = jnp.minimum(jnp.maximum(z - off_ref[0, s], -1), BZ) + 1
             starts.append(s * rim + a * rim_y)
         for y in range(fy):
             low = jnp.zeros((cols, 128), F32)
             high = low
             for s in range(slots):
-                b = jnp.minimum(jnp.maximum(y - off_ref[slots + s], -1), BY) + 1
+                b = jnp.minimum(jnp.maximum(y - off_ref[1, s], -1), BY) + 1
                 low = low + pieces[starts[s] + b, 0]
                 high = high + pieces[starts[s] + b, 1]
             nf[z, y] = low
@@ -341,7 +355,6 @@
                     tile = jnp.where(keep, pltpu.roll(value, 16 * j, 1) if j else value, tile)
                 spack[filled + q] = tile
             filled += tiles_of(len(cells))
-    more_z, more_y = fz - cz, fy - cy
     sends = [
         (nf.at[pl.ds(cz, more_z), pl.ds(0, cy)], rz, (1, 0, 0)),
         (nf.at[pl.ds(0, cz), pl.ds(cy, more_y)], ry, (0, 1, 0)),
@@ -352,23 +365,31 @@
         sends.append((spack.at[part], rx.at[part], (up_z, up_y, 1)))
     copies = launch(sends, spill_send, spill_recv)
 
+    for copy in late_copies:
+        copy.wait()
+    for cell in range(own):
+        turn = (112 - 16 * (cell % 8)) % 128
+        left = xl[cell // 8]
+        left = pltpu.roll(left, turn, 1) if turn else left
+        halo_x[cell] = jnp.where(lane < 64, frame_x[cell // cy * fy + cell % cy], left)
+
     @pl.loop(0, cz)
     def _(z):
         for y in range(cy):
             cell = z * cy + y
-            centre = zext[own + cell]
+            centre = zext[cz + z, y]
             edge = halo_x[cell]
-            vv = v_ref[cell]
+            vv = v_ref[z, y : y + 1, :]
             total = centre * (vv - 1.5 * LAP_CENTER)
             for k, weight in enumerate(LAP_COEFFS, start=1):
-                beside = zext[own + cell + k * cy] + zext[own + cell - k * cy]
+                beside = zext[cz + z + k, y] + zext[cz + z - k, y]
                 for target in (y + k, y - k):
                     if target >= cy:
-                        beside = beside + ybuf[1, z * cy + target - cy]
+                        beside = beside + ybuf[1, z, target - cy]
                     elif target < 0:
-                        beside = beside + ybuf[below_y, z * cy + target + cy]
+                        beside = beside + ybuf[below_y, z, target + cy]
                     else:
-                        beside = beside + zext[own + z * cy + target]
+                        beside = beside + zext[cz + z, target]
                 beside = beside + pltpu.roll(jnp.where(lane < k, edge, centre), 128 - k, 1)
                 beside = beside + pltpu.roll(jnp.where(lane >= 128 - k, edge, centre), k, 1)
                 total = total - 0.5 * weight * beside
@@ -401,7 +422,41 @@
 
     hw_row = products(HW, XX, HW + 1)
     second = jnp.where(lane < 96, hw_row, pltpu.roll(w_row2_pad(w_row2), 32, 1))
-    red2_ref[...] = finish(reduced(1, jnp.concatenate([w_row, second], 0)))
+    sums2 = finish(reduced(1, paired(w_row, second)))
+    weight = 1.0 / (own * cx * nz * ny * nx)
+    sums1 = red1_ref[...]
+    rows = jnp.concatenate([sums1, pltpu.roll(sums1, 112, 1), sums2, pltpu.roll(sums2, 112, 1)], 0)
+    rows = rows * weight
+    turned = jnp.transpose(jnp.concatenate([rows, jnp.zeros_like(rows)], 0))
+
+    def direct(row, group, target):
+        return rows[16 * row : 16 * row + 16, :], 32 * group, target
+
+    def flipped(row, group, target):
+        return turned[32 * group : 32 * group + 16, :], 16 * row, target
+
+    def laid(parts):
+        total = None
+        for tile, begin, target in parts:
+            shift = (16 * target - begin) % 128
+            tile = pltpu.roll(tile, shift, 1) if shift else tile
+            tile = jnp.where((lane >= 16 * target) & (lane < 16 * target + 16), tile, 0.0)
+            total = tile if total is None else total + tile
+        return total
+
+    gram = [
+        [direct(0, 2, 0), flipped(2, 2, 1), direct(0, 3, 2)],
+        [direct(2, 2, 0), direct(3, 3, 1), direct(2, 3, 2)],
+        [direct(1, 2, 0), flipped(2, 3, 1), direct(1, 3, 2)],
+    ]
+    rayleigh = [
+        [flipped(0, 1, 0), flipped(3, 0, 1), direct(0, 0, 2)],
+        [direct(2, 1, 0), flipped(3, 2, 1), direct(2, 0, 2)],
+        [direct(1, 1, 0), flipped(3, 1, 1), direct(1, 0, 2)],
+    ]
+    for i in range(3):
+        gram_ref[16 * i : 16 * i + 16, :] = laid(gram[i])[:, :48]
+        ray_ref[16 * i : 16 * i + 16, :] = laid(rayleigh[i])[:, :48]
 
 
 def w_row2_pad(row):
@@ -418,11 +473,6 @@
     nz, ny, nx = sizes
     own = cz * cy
     fz, fy = cz + BZ - 1, cy + BY - 1
-    beta = masked_projectors(projectors, atom_count, proj_count, extents)[0, 0, 0]
-    beta = beta.reshape(slots, nproj, BZ * BY, BX).transpose(0, 2, 1, 3)
-    beta = beta.reshape(slots * BZ * BY * nproj, BX)
-    beta = jnp.pad(beta, ((0, 0), (0, 128 - BX)))
-    sym = (0.5 * (coupling + jnp.swapaxes(coupling, -1, -2))).reshape(-1)
     turned = [
         jnp.transpose(b, (1, 2, 0, 3)).reshape(own, cols, cx)
         for b in (block_x, block_hx, block_p, block_hp)
@@ -442,10 +492,11 @@
     )
     per_slot = BZ * BY * nproj
     scratch = [
+        pltpu.VMEM((cols, 128), F32),
         pltpu.VMEM((192, own * 128), BF16),
-        pltpu.VMEM((3 * own,) + tile, F32),
-        pltpu.VMEM((2, own) + tile, F32),
-        pltpu.VMEM(((BZ - 1) * cy,) + tile, F32),
+        pltpu.VMEM((3 * cz, cy) + tile, F32),
+        pltpu.VMEM((2, cz, cy) + tile, F32),
+        pltpu.VMEM((BZ - 1, BY - 1) + tile, F32),
         pltpu.VMEM((tiles_of(own),) + tile, F32),
         pltpu.VMEM((tiles_of(own),) + tile, F32),
         pltpu.VMEM((4, tiles_of(own)) + tile, F32),
@@ -465,50 +516,32 @@
         pltpu.VMEM((packed,) + tile, F32),
         pltpu.VMEM((8, 128), F32),
     ]
-    scratch += [pltpu.VMEM((t, 2 * cols, 128), F32) for t in totals] * 2
+    scratch += [pltpu.VMEM((t, cols, 128), F32) for t in totals] * 2
     scratch += [
         pltpu.SemaphoreType.DMA((2 * sum(totals),)),
         pltpu.SemaphoreType.DMA((2 * sum(totals),)),
-        pltpu.SemaphoreType.DMA((10,)),
-        pltpu.SemaphoreType.DMA((10,)),
+        pltpu.SemaphoreType.DMA((12,)),
+        pltpu.SemaphoreType.DMA((12,)),
         pltpu.SemaphoreType.DMA((7,)),
         pltpu.SemaphoreType.DMA((7,)),
     ]
     vmem = pl.BlockSpec(memory_space=pltpu.VMEM)
     smem = pl.BlockSpec(memory_space=pltpu.SMEM)
-    w, hw, red1, red2 = pl.pallas_call(
+    w, hw, gram, rayleigh = pl.pallas_call(
         functools.partial(kernel, sizes, groups, (cz, cy, cx, slots, nproj, cols)),
         out_shape=(
             jax.ShapeDtypeStruct((own,) + tile, F32),
             jax.ShapeDtypeStruct((own,) + tile, F32),
-            jax.ShapeDtypeStruct((2 * cols, 128), F32),
-            jax.ShapeDtypeStruct((2 * cols, 128), F32),
+            jax.ShapeDtypeStruct((3 * cols, 3 * cols), F32),
+            jax.ShapeDtypeStruct((3 * cols, 3 * cols), F32),
         ),
-        in_specs=[smem, smem] + [vmem] * 6,
+        in_specs=[smem] * 5 + [vmem] * 6,
         out_specs=(vmem,) * 4,
         scratch_shapes=scratch,
         compiler_params=pltpu.CompilerParams(collective_id=0, has_side_effects=True),
-    )(offsets.reshape(-1), sym, *turned, potential.reshape(own, 1, cx), beta)
-    weight = 1.0 / (own * cx * nz * ny * nx)
-
-    def block(rows, group):
-        start = 32 * group
-        return (rows[:, start : start + cols] + rows[:, start + cols : start + 2 * cols]) * weight
-
-    x_row, p_row, w_row, hw_row = red1[:cols], red1[cols:], red2[:cols], red2[cols:]
-    gram = jnp.block(
-        [
-            [block(x_row, 2), block(w_row, 2).T, block(x_row, 3)],
-            [block(w_row, 2), block(hw_row, 3), block(w_row, 3)],
-            [block(p_row, 2), block(w_row, 3).T, block(p_row, 3)],
-        ]
-    )
-    rayleigh = jnp.block(
-        [
-            [block(x_row, 0).T, block(hw_row, 0).T, block(x_row, 1)],
-            [block(w_row, 0), block(hw_row, 2).T, block(w_row, 1)],
-            [block(p_row, 0), block(hw_row, 1).T, block(p_row, 1)],
-        ]
+    )(
+        offsets[:, 0, 0, 0], extents[:, 0, 0, 0], atom_count[0], proj_count[0, 0], coupling[0, 0, 0],
+        *turned, potential, projectors[0, 0, 0],
     )
     w, hw = (jnp.transpose(b.reshape(cz, cy, cols, cx), (2, 0, 1, 3)) for b in (w, hw))
     return (w, hw, gram, rayleigh)

time: 64.9 us -> 51.9 us (0.80)
  Pallas kernels: 51.7 us -> 44.4 us
  other arithmetic: 2.88 us -> 0 us
  local copies, waits for them, and re-layouts: 8.37 us -> 5.79 us
    pallas_call x1, Pallas kernels: 51.7 us -> 44.4 us  [per_device(): pl.pallas_call(functools.partial(kernel, sizes, groups, (cz, cy, cx, slot...]
    reshape x3 -> x0, local copies, waits for them, and re-layouts: 1.84 us -> none  [the longest x1 0.62 us: per_device(): potential.reshape(own, 1, cx)]
    concatenate x2 -> x0, other arithmetic: 1.39 us -> none  [the longest x1 0.69 us: per_device(): jnp.block([[block(x_row, 2), block(w_row, 2).T, block(x_row, 3)], [block(...]
    transpose x3 -> x0, other arithmetic: 1.22 us -> none  [the longest x1 1.12 us: per_device(): block(hw_row, 0)]
    pad x1 -> x0, local copies, waits for them, and re-layouts: 0.72 us -> none  [per_device(): beta = jnp.pad(beta, ((0, 0), (0, 128 - BX)))]
    squeeze x0 -> x1, local copies, waits for them, and re-layouts: none -> 0.7 us  [per_device(): coupling[0, 0, 0]]
    unnamed x22 -> x17, local copies, waits for them, and re-layouts: 4.94 us -> 5.09 us
where the time goes in v2:
time: 51.9 us; the launch traced here: 51.6 us
  Pallas kernels  44.4 us (86%)
  local copies, waits for them, and re-layouts  5.79 us (11%)
  between operations  1.32 us (3%)
    pallas_call x1, Pallas kernels, per_device(): pl.pallas_call(functools.partial(kernel, sizes, groups, (cz, cy, cx, slot...  44.4 us
    unnamed x17, local copies, waits for them, and re-layouts  5.09 us

profile of v2, /device:TPU:0, one launch (start us, length us, event | category | flops | bytes accessed | tf_op | source)
XLA Modules:
  0.0 51.6 jit_solution(15402809567234883886)
XLA Ops:
  1.3 0.0 copy-start.4
  1.3 0.0 copy-start.5
  1.3 0.0 copy-start.3
  1.3 0.7 %copy-done.4 = s32[3,1,1,1,8]{4,3,2,1,0:T(1,128)S(1)} copy-done((s32[3,1,1,1,8]{4,3,2,1,0:T(1,128)S(1)}, s32[3,1,1,1,8]{4,3,2,1,0:T(1,128)}, u32[]{:S(2)}) %copy-start.4) | copy-done | bytes 120
  2.0 0.0 copy-done.5
  2.0 0.6 %copy_bitcast_fusion = (s32[3,8]{1,0:T(4,128)}, s32[3,8]{1,0:T(4,128)}) fusion(s32[3,1,1,1,8]{4,3,2,1,0:T(1,128)S(1)} %copy-done.4, s32[3,1,1,1,8]{4,3,2,1,0:T(1,128)S(1)} %copy-done.5), kind=kLoop, calls=%fused_computation | loop fusion | bytes 384
  2.6 0.0 copy-done.3
  2.6 0.7 %copy.15.d_ref = f32[8,4,4]{2,1,0:T(4,128)} copy(f32[8,4,4]{0,2,1:T(4,128)S(1)} %bitcast.34) | data formatting | bytes 1024 | tf_op jit(solution)/shard_map/squeeze | solution.py:543
  3.3 44.4 %shard_map.138 = (f32[36,16,128]{2,1,0:T(8,128)}, f32[36,16,128]{2,1,0:T(8,128)}, f32[48,48]{1,0:T(8,128)}, f32[48,48]{1,0:T(8,128)}) custom-call(s32[3,8]{1,0:T(4,128)} %get-tuple-element.13.off_ref, s32[3,8]{1,0:T(4,128)} %get-tuple-element.12.ext_ref, s32[1,1]{1,0:T(1,128)} %bitcast.26.count_ref, s32[1,8]{1,0:T(1,128)} %bitcast.35, ...), custom_call_target="tpu_custom_call" | custom-call | tf_op jit(solution)/shard_map/pallas_call | solution.py:530
  47.7 0.0 copy-start
  47.7 1.7 %copy.25 = f32[16,6,6,128]{3,0,2,1:T(8,128)} copy(f32[16,6,6,128]{3,0,2,1:T(8,128)} %bitcast.28) | data formatting | bytes 589824
  49.5 0.0 copy-done
  49.5 0.0 copy-start.2
  49.5 0.7 %copy.26 = f32[16,6,6,128]{3,0,2,1:T(8,128)} copy(f32[16,6,6,128]{3,0,2,1:T(8,128)S(1)} %bitcast.27) | data formatting | bytes 589824
  50.2 0.0 copy-done.2
  50.2 0.0 copy-start.1
  50.2 0.6 %copy.27 = f32[48,48]{1,0:T(8,128)} copy(f32[48,48]{1,0:T(8,128)S(1)} %copy-done.2) | data formatting | bytes 18432
  50.8 0.1 copy-done.1
  50.9 0.6 %copy.28 = f32[48,48]{1,0:T(8,128)} copy(f32[48,48]{1,0:T(8,128)S(1)} %copy-done.1) | data formatting | bytes 18432
Async XLA Ops:
  1.3 0.7 %copy-start.4 = (s32[3,1,1,1,8]{4,3,2,1,0:T(1,128)S(1)}, s32[3,1,1,1,8]{4,3,2,1,0:T(1,128)}, u32[]{:S(2)}) copy-start(s32[3,1,1,1,8]{4,3,2,1,0:T(1,128)} %param.21) | copy-start | bytes 292
  1.3 0.7 %copy-start.5 = (s32[3,1,1,1,8]{4,3,2,1,0:T(1,128)S(1)}, s32[3,1,1,1,8]{4,3,2,1,0:T(1,128)}, u32[]{:S(2)}) copy-start(s32[3,1,1,1,8]{4,3,2,1,0:T(1,128)} %param.20) | copy-start | bytes 292
  1.3 1.3 %copy-start.3 = (f32[1,1,1,8,4,4]{3,5,4,2,1,0:T(4,128)S(1)}, f32[1,1,1,8,4,4]{3,5,4,2,1,0:T(4,128)}, u32[]{:S(2)}) copy-start(f32[1,1,1,8,4,4]{3,5,4,2,1,0:T(4,128)} %param.17) | copy-start | bytes 1540
  47.7 1.8 %copy-start = (f32[36,16,128]{2,1,0:T(8,128)S(1)}, f32[36,16,128]{2,1,0:T(8,128)}, u32[]{:S(2)}) copy-start(f32[36,16,128]{2,1,0:T(8,128)} %get-tuple-element.9) | copy-start | bytes 884740
  49.5 0.7 %copy-start.2 = (f32[48,48]{1,0:T(8,128)S(1)}, f32[48,48]{1,0:T(8,128)}, u32[]{:S(2)}) copy-start(f32[48,48]{1,0:T(8,128)} %get-tuple-element.20) | copy-start | bytes 27652
  50.2 0.7 %copy-start.1 = (f32[48,48]{1,0:T(8,128)S(1)}, f32[48,48]{1,0:T(8,128)}, u32[]{:S(2)}) copy-start(f32[48,48]{1,0:T(8,128)} %get-tuple-element.21) | copy-start | bytes 27652

commit v3 on v2

--- a/solution.py
+++ b/solution.py
@@ -23,7 +23,7 @@
 
 def kernel(
     sizes, groups, dims,
-    off_ref, ext_ref, count_ref, proj_ref, d_ref, x_ref, hx_ref, p_ref, hp_ref, v_ref, beta_ref,
+    off_ref, ext_ref, count_ref, proj_ref, d_ref, x_in, hx_in, p_in, hp_in, v_ref, beta_ref,
     w_ref, hw_ref, gram_ref, ray_ref, red1_ref,
     stack, zext, ybuf, zybuf, plow, phigh, xr, xl, frame, frame_x, halo_x,
     blo, bhi, pieces, nf, nh, spack, rz, ry, rzy, rx, wout,
@@ -34,7 +34,14 @@
     n_red = len(groups)
     bufs = (rest[:n_red], rest[n_red : 2 * n_red])
     rest = rest[2 * n_red :]
-    red_send, red_recv, halo_send, halo_recv, spill_send, spill_recv = rest
+    red_send, red_recv, halo_send, halo_recv, spill_send, spill_recv = rest[:6]
+    load_sem, x_ref, hx_ref, p_ref, hp_ref = rest[6:]
+    loads = []
+    for i, (source, target) in enumerate(
+        ((x_in, x_ref), (hx_in, hx_ref), (p_in, p_ref), (hp_in, hp_ref))
+    ):
+        loads.append(pltpu.make_async_copy(source, target, load_sem.at[i]))
+        loads[-1].start()
     zi, yi, xi = (lax.axis_index(a) for a in AXES)
     size_of = dict(zip(AXES, sizes))
     here = dict(zip(AXES, (zi, yi, xi)))
@@ -82,6 +89,9 @@
         low = (value - high.astype(F32)).astype(BF16)
         start = cell * 128 if isinstance(cell, int) else pl.multiple_of(cell * 128, 128)
         stack[kind * 32 : kind * 32 + 32, pl.ds(start, 128)] = jnp.concatenate([high, low], 0)
+
+    for load in loads:
+        load.wait()
 
     @pl.loop(0, cz)
     def _(z):
@@ -184,10 +194,17 @@
     matrix = jnp.concatenate([pltpu.roll(sums1, 64, 1), pltpu.roll(sums1, 96, 1)], 0)
     lane2 = lax.broadcasted_iota(jnp.int32, (2 * cols, 128), 1)
     matrix = jnp.where(lane2 < cols, matrix, 0.0)
-    for k in range(cols):
-        row = matrix[k : k + 1, :]
-        column = matrix[:, k : k + 1] / matrix[k : k + 1, k : k + 1]
-        matrix = jnp.where(lane2 == k, column, matrix - column * row)
+    for k in range(0, cols, 2):
+        row0, row1 = matrix[k : k + 1, :], matrix[k + 1 : k + 2, :]
+        col0, col1 = matrix[:, k : k + 1], matrix[:, k + 1 : k + 2]
+        a, b = matrix[k : k + 1, k : k + 1], matrix[k : k + 1, k + 1 : k + 2]
+        c, d = matrix[k + 1 : k + 2, k : k + 1], matrix[k + 1 : k + 2, k + 1 : k + 2]
+        ratio = c / a
+        schur = d - ratio * b
+        new1 = (col1 - col0 * (b / a)) / schur
+        new0 = col0 / a - new1 * ratio
+        rest_of = matrix - new0 * row0 - new1 * row1
+        matrix = jnp.where(lane2 == k, new0, jnp.where(lane2 == k + 1, new1, rest_of))
     theta_t = matrix[cols:, :]
     theta_cols = [jnp.broadcast_to(theta_t[:, k : k + 1], (cols, 128)) for k in range(cols)]
 
@@ -303,11 +320,12 @@
                     )
         overlaps = [jnp.broadcast_to(jnp.sum(v, axis=1, keepdims=True), (cols, 128)) for v in sums]
         outs = []
+        dm = d_ref[s]
         for p in range(nproj):
-            value = overlaps[p] * d_ref[s, p, p]
+            value = overlaps[p] * dm[p : p + 1, p : p + 1]
             for q in range(nproj):
                 if q != p:
-                    value = value + overlaps[q] * (0.5 * (d_ref[s, p, q] + d_ref[s, q, p]))
+                    value = value + overlaps[q] * (0.5 * (dm[p : p + 1, q : q + 1] + dm[q : q + 1, p : p + 1]))
             outs.append(value)
         for a in range(BZ):
             for b in range(BY):
@@ -457,6 +475,12 @@
     for i in range(3):
         gram_ref[16 * i : 16 * i + 16, :] = laid(gram[i])[:, :48]
         ray_ref[16 * i : 16 * i + 16, :] = laid(rayleigh[i])[:, :48]
+
+
+def put_out(*refs):
+    half = len(refs) // 2
+    for source, target in zip(refs[:half], refs[half:]):
+        target[...] = source[...]
 
 
 def w_row2_pad(row):
@@ -524,7 +548,9 @@
         pltpu.SemaphoreType.DMA((12,)),
         pltpu.SemaphoreType.DMA((7,)),
         pltpu.SemaphoreType.DMA((7,)),
-    ]
+        pltpu.SemaphoreType.DMA((4,)),
+    ]
+    scratch += [pltpu.VMEM((own,) + tile, F32)] * 4
     vmem = pl.BlockSpec(memory_space=pltpu.VMEM)
     smem = pl.BlockSpec(memory_space=pltpu.SMEM)
     w, hw, gram, rayleigh = pl.pallas_call(
@@ -535,7 +561,7 @@
             jax.ShapeDtypeStruct((3 * cols, 3 * cols), F32),
             jax.ShapeDtypeStruct((3 * cols, 3 * cols), F32),
         ),
-        in_specs=[smem] * 5 + [vmem] * 6,
+        in_specs=[smem] * 4 + [vmem] + [pl.BlockSpec(memory_space=pl.ANY)] * 4 + [vmem] * 2,
         out_specs=(vmem,) * 4,
         scratch_shapes=scratch,
         compiler_params=pltpu.CompilerParams(collective_id=0, has_side_effects=True),
@@ -543,6 +569,12 @@
         offsets[:, 0, 0, 0], extents[:, 0, 0, 0], atom_count[0], proj_count[0, 0], coupling[0, 0, 0],
         *turned, potential, projectors[0, 0, 0],
     )
+    w, hw, gram, rayleigh = pl.pallas_call(
+        put_out,
+        out_shape=tuple(jax.ShapeDtypeStruct(b.shape, F32) for b in (w, hw, gram, rayleigh)),
+        in_specs=[vmem] * 4,
+        out_specs=(vmem,) * 4,
+    )(w, hw, gram, rayleigh)
     w, hw = (jnp.transpose(b.reshape(cz, cy, cols, cx), (2, 0, 1, 3)) for b in (w, hw))
     return (w, hw, gram, rayleigh)
 

time: 51.9 us -> 51 us (0.983)
  local copies, waits for them, and re-layouts: 5.79 us -> 1.96 us
  Pallas kernels: 44.4 us -> 47.5 us
    unnamed x17 -> x7, local copies, waits for them, and re-layouts: 5.09 us -> 1.26 us
    pallas_call x0 -> x1, Pallas kernels: none -> 1.89 us  [per_device(): pl.pallas_call(put_out, out_shape=tuple((jax.ShapeDtypeStruct(b.shape, F3...]
    pallas_call x1, Pallas kernels: 44.4 us -> 45.6 us  [per_device(): pl.pallas_call(functools.partial(kernel, sizes, groups, (cz, cy, cx, slot...]
where the time goes in v3:
time: 51 us; the launch traced here: 50.7 us
  Pallas kernels  47.5 us (93%)
  local copies, waits for them, and re-layouts  1.96 us (4%)
  between operations  1.31 us (3%)
    pallas_call x1, Pallas kernels, per_device(): pl.pallas_call(functools.partial(kernel, sizes, groups, (cz, cy, cx, slot...  45.6 us
    pallas_call x1, Pallas kernels, per_device(): pl.pallas_call(put_out, out_shape=tuple((jax.ShapeDtypeStruct(b.shape, F3...  1.89 us
    unnamed x7, local copies, waits for them, and re-layouts  1.26 us

profile of v3, /device:TPU:0, one launch (start us, length us, event | category | flops | bytes accessed | tf_op | source)
XLA Modules:
  0.0 50.7 jit_solution(14577754390687812320)
XLA Ops:
  1.3 0.0 copy-start.1
  1.3 0.0 copy-start.2
  1.3 0.0 copy-start
  1.3 0.7 %copy-done.1 = s32[3,1,1,1,8]{4,3,2,1,0:T(1,128)S(1)} copy-done((s32[3,1,1,1,8]{4,3,2,1,0:T(1,128)S(1)}, s32[3,1,1,1,8]{4,3,2,1,0:T(1,128)}, u32[]{:S(2)}) %copy-start.1) | copy-done | bytes 120
  2.0 0.0 copy-done.2
  2.0 0.6 %copy_bitcast_fusion = (s32[3,8]{1,0:T(4,128)}, s32[3,8]{1,0:T(4,128)}) fusion(s32[3,1,1,1,8]{4,3,2,1,0:T(1,128)S(1)} %copy-done.1, s32[3,1,1,1,8]{4,3,2,1,0:T(1,128)S(1)} %copy-done.2), kind=kLoop, calls=%fused_computation | loop fusion | bytes 384
  2.6 0.0 copy-done
  2.6 0.7 %copy.15.d_ref = f32[8,4,4]{2,1,0:T(4,128)} copy(f32[8,4,4]{0,2,1:T(4,128)S(1)} %bitcast.32) | data formatting | bytes 1024 | tf_op jit(solution)/shard_map/squeeze | solution.py:569
  3.3 45.6 %shard_map.138 = (f32[36,16,128]{2,1,0:T(8,128)}, f32[36,16,128]{2,1,0:T(8,128)}, f32[48,48]{1,0:T(8,128)}, f32[48,48]{1,0:T(8,128)}) custom-call(s32[3,8]{1,0:T(4,128)} %get-tuple-element.21.off_ref, s32[3,8]{1,0:T(4,128)} %get-tuple-element.20.ext_ref, s32[1,1]{1,0:T(1,128)} %bitcast.26.count_ref, s32[1,8]{1,0:T(1,128)} %bitcast.33, ...), custom_call_target="tpu_custom_call" | custom-call | tf_op jit(solution)/shard_map/pallas_call | solution.py:556
  48.9 1.9 %shard_map.139 = (f32[36,16,128]{2,1,0:T(8,128)}, f32[36,16,128]{2,1,0:T(8,128)}, f32[48,48]{1,0:T(8,128)}, f32[48,48]{1,0:T(8,128)}) custom-call(f32[36,16,128]{2,1,0:T(8,128)} %get-tuple-element.12.refs_0_, f32[36,16,128]{2,1,0:T(8,128)} %get-tuple-element.13.refs_1_, f32[48,48]{1,0:T(8,128)} %get-tuple-element.14.refs_2_, f32[48,48]{1,0:T(8,128)} %get-tuple-element.15.refs_3_), custom_call_target="tpu_custom_call" | custom-call | tf_op jit(solution)/shard_map/pallas_call | solution.py:572
Async XLA Ops:
  1.3 0.7 %copy-start.1 = (s32[3,1,1,1,8]{4,3,2,1,0:T(1,128)S(1)}, s32[3,1,1,1,8]{4,3,2,1,0:T(1,128)}, u32[]{:S(2)}) copy-start(s32[3,1,1,1,8]{4,3,2,1,0:T(1,128)} %param.21) | copy-start | bytes 292
  1.3 0.7 %copy-start.2 = (s32[3,1,1,1,8]{4,3,2,1,0:T(1,128)S(1)}, s32[3,1,1,1,8]{4,3,2,1,0:T(1,128)}, u32[]{:S(2)}) copy-start(s32[3,1,1,1,8]{4,3,2,1,0:T(1,128)} %param.20) | copy-start | bytes 292
  1.3 1.3 %copy-start = (f32[1,1,1,8,4,4]{3,5,4,2,1,0:T(4,128)S(1)}, f32[1,1,1,8,4,4]{3,5,4,2,1,0:T(4,128)}, u32[]{:S(2)}) copy-start(f32[1,1,1,8,4,4]{3,5,4,2,1,0:T(4,128)} %param.17) | copy-start | bytes 1540

commit v4 on v3

--- a/solution.py
+++ b/solution.py
@@ -164,15 +164,15 @@
     row_p = lax.broadcasted_iota(jnp.int32, (nproj, 128), 0)
     in_tile = 128 // BX
     for s in range(slots):
-        ox = off_ref[2, s]
+        ox = off_ref[2, 0, 0, 0, s]
         along = lax.rem(lane_p - ox + 128, 128)
         along = jnp.where(row_p < proj_ref[0, s], along, 128)
         low_side = lane_p >= ox
         live = s < count_ref[0, 0]
         for a in range(BZ):
             for b in range(BY):
-                used = live & (a < ext_ref[0, s]) & (b < ext_ref[1, s])
-                limit = jnp.where(used, jnp.minimum(ext_ref[2, s], BX), 0)
+                used = live & (a < ext_ref[0, 0, 0, 0, s]) & (b < ext_ref[1, 0, 0, 0, s])
+                limit = jnp.where(used, jnp.minimum(ext_ref[2, 0, 0, 0, s], BX), 0)
                 box = a * BY + b
                 part = beta_ref[s, :, (box // in_tile) * 128 : (box // in_tile) * 128 + 128]
                 part = pltpu.roll(part, lax.rem(ox + 128 - BX * (box % in_tile), 128), 1)
@@ -306,7 +306,7 @@
 
     @pl.loop(0, slots)
     def _(s):
-        oz, oy = off_ref[0, s], off_ref[1, s]
+        oz, oy = off_ref[0, 0, 0, 0, s], off_ref[1, 0, 0, 0, s]
         sums = [jnp.zeros((cols, 128), F32) for _ in range(nproj)]
         for a in range(BZ):
             for b in range(BY):
@@ -320,7 +320,7 @@
                     )
         overlaps = [jnp.broadcast_to(jnp.sum(v, axis=1, keepdims=True), (cols, 128)) for v in sums]
         outs = []
-        dm = d_ref[s]
+        dm = d_ref[0, 0, 0, s]
         for p in range(nproj):
             value = overlaps[p] * dm[p : p + 1, p : p + 1]
             for q in range(nproj):
@@ -343,13 +343,13 @@
     def _(z):
         starts = []
         for s in range(slots):
-            a = jnp.minimum(jnp.maximum(z - off_ref[0, s], -1), BZ) + 1
+            a = jnp.minimum(jnp.maximum(z - off_ref[0, 0, 0, 0, s], -1), BZ) + 1
             starts.append(s * rim + a * rim_y)
         for y in range(fy):
             low = jnp.zeros((cols, 128), F32)
             high = low
             for s in range(slots):
-                b = jnp.minimum(jnp.maximum(y - off_ref[1, s], -1), BY) + 1
+                b = jnp.minimum(jnp.maximum(y - off_ref[1, 0, 0, 0, s], -1), BY) + 1
                 low = low + pieces[starts[s] + b, 0]
                 high = high + pieces[starts[s] + b, 1]
             nf[z, y] = low
@@ -566,7 +566,7 @@
         scratch_shapes=scratch,
         compiler_params=pltpu.CompilerParams(collective_id=0, has_side_effects=True),
     )(
-        offsets[:, 0, 0, 0], extents[:, 0, 0, 0], atom_count[0], proj_count[0, 0], coupling[0, 0, 0],
+        offsets, extents, atom_count[0], proj_count[0, 0], coupling,
         *turned, potential, projectors[0, 0, 0],
     )
     w, hw, gram, rayleigh = pl.pallas_call(

time: 51 us -> 49.8 us (0.976)
  local copies, waits for them, and re-layouts: 1.96 us -> 0.73 us
    squeeze x1 -> x0, local copies, waits for them, and re-layouts: 0.7 us -> none  [per_device(): coupling[0, 0, 0]]
    unnamed x7 -> x3, local copies, waits for them, and re-layouts: 1.26 us -> 0.73 us
where the time goes in v4:
time: 49.8 us; the launch traced here: 49.5 us
  Pallas kernels  47.4 us (95%)
  between operations  1.31 us (3%)
  local copies, waits for them, and re-layouts  0.73 us (1%)
    pallas_call x1, Pallas kernels, per_device(): pl.pallas_call(functools.partial(kernel, sizes, groups, (cz, cy, cx, slot...  45.6 us
    pallas_call x1, Pallas kernels, per_device(): pl.pallas_call(put_out, out_shape=tuple((jax.ShapeDtypeStruct(b.shape, F3...  1.89 us

profile of v4, /device:TPU:0, one launch (start us, length us, event | category | flops | bytes accessed | tf_op | source)
XLA Modules:
  0.0 49.5 jit_solution(12919950887355030190)
XLA Ops:
  0.6 0.0 copy-start
  1.3 0.0 copy-done
  1.3 0.7 %copy.15.d_ref = f32[1,1,1,8,4,4]{5,4,3,2,1,0:T(4,128)} copy(f32[1,1,1,8,4,4]{3,5,4,2,1,0:T(4,128)S(1)} %copy-done) | data formatting | bytes 1024 | tf_op args[6]
  2.0 45.6 %shard_map.138 = (f32[36,16,128]{2,1,0:T(8,128)}, f32[36,16,128]{2,1,0:T(8,128)}, f32[48,48]{1,0:T(8,128)}, f32[48,48]{1,0:T(8,128)}) custom-call(s32[3,1,1,1,8]{4,3,2,1,0:T(1,128)} %off_ref.1, s32[3,1,1,1,8]{4,3,2,1,0:T(1,128)} %ext_ref.1, s32[1,1]{1,0:T(1,128)} %bitcast.21.count_ref, s32[1,8]{1,0:T(1,128)} %bitcast.27, f32[1,1,1,8,4,4]{5,4,3,2,1,0:T(4,128)} %copy.15.d_ref, ...), custom_call_target="tpu_custom_call" | custom-call | tf_op jit(solution)/shard_map/pallas_call | solution.py:556
  47.6 1.9 %shard_map.139 = (f32[36,16,128]{2,1,0:T(8,128)}, f32[36,16,128]{2,1,0:T(8,128)}, f32[48,48]{1,0:T(8,128)}, f32[48,48]{1,0:T(8,128)}) custom-call(f32[36,16,128]{2,1,0:T(8,128)} %get-tuple-element.12.refs_0_, f32[36,16,128]{2,1,0:T(8,128)} %get-tuple-element.13.refs_1_, f32[48,48]{1,0:T(8,128)} %get-tuple-element.14.refs_2_, f32[48,48]{1,0:T(8,128)} %get-tuple-element.15.refs_3_), custom_call_target="tpu_custom_call" | custom-call | tf_op jit(solution)/shard_map/pallas_call | solution.py:572
Async XLA Ops:
  0.6 0.7 %copy-start = (f32[1,1,1,8,4,4]{3,5,4,2,1,0:T(4,128)S(1)}, f32[1,1,1,8,4,4]{3,5,4,2,1,0:T(4,128)}, u32[]{:S(2)}) copy-start(f32[1,1,1,8,4,4]{3,5,4,2,1,0:T(4,128)} %param.17) | copy-start | bytes 1540
